TPU v7x, 256 devices: a whole 4x4x8 slice. The times are simulated.
256 devices in a mesh: ba: 8 (over z), aa: 32 (over x, y, core).
Axes of the slice: x: 4, y: 4, z: 8, core: 2. Of those that a mesh axis runs over, the one named last changes fastest.
Arguments:
- tokens: bfloat16 [49152, 1024], P(('ba', 'aa')), parts along dimension 0, may hold values from -6 to 6
- latents: bfloat16 [8192, 1024], P(('ba', 'aa')), parts along dimension 0, may hold values from -6 to 6
- read_query: bfloat16 [1024, 512], replicated, may hold values from -0.1875 to 0.1875
- read_keyval: bfloat16 [1024, 1024], replicated, may hold values from -0.1875 to 0.1875
- read_out: bfloat16 [512, 1024], replicated, may hold values from -0.25 to 0.25
- self_qkv: bfloat16 [1024, 1536], replicated, may hold values from -0.1875 to 0.1875
- self_out: bfloat16 [512, 1024], replicated, may hold values from -0.25 to 0.25
- write_query: bfloat16 [1024, 512], replicated, may hold values from -0.1875 to 0.1875
- write_keyval: bfloat16 [1024, 1024], replicated, may hold values from -0.1875 to 0.1875
- write_out: bfloat16 [512, 1024], replicated, may hold values from -0.25 to 0.25
- qk_gain: float32 [6, 512], replicated, may hold values from 0.8 to 2.2
Outputs:
- tokens_out: bfloat16 [49152, 1024], P(('ba', 'aa')), parts along dimension 0
- latents_out: bfloat16 [8192, 1024], P(('ba', 'aa')), parts along dimension 0
There are 8 independent parts, one for each index of `ba`. A program takes and returns all parts, laid end to end along the dimension named above; an argument that names none is the same for every part. Nothing has to cross between parts.
All inputs are finite; a program needn't handle non-finite values.
Results may differ from a plain program's by a relative error of at most 0.014.
Values may be sent and summed in bfloat16 or wider, within the bound.
No kernel may reach another device: no remote copies, remote signals or barrier semaphores. Data moves between devices by JAX's collectives and lax.ppermute only.
A program may use at most 64 MiB of HBM per device.

v0:
```python
import math

import jax
import jax.numpy as jnp
from jax import lax
from jax.experimental import pallas as pl
from jax.experimental.pallas import tpu as pltpu
from jax.sharding import Mesh
from jax.sharding import PartitionSpec as P


AA = ("aa_0", "aa_1", "aa_2")
BA_AA = ("ba", "aa_0", "aa_1", "aa_2")
HEADS = 8
PAIRS = 4
EPSILON = 1e-06
QUERY_SCALE = math.log2(math.e) / 8.0
F32, BF16 = jnp.float32, jnp.bfloat16


def own_pair():
    return 2 * lax.rem(lax.axis_index("aa_1"), 2) + lax.axis_index("aa_2")


def to_peer(x, k):
    swaps = [(i, i ^ k) for i in range(8)]
    return lax.ppermute(x, ("aa_1", "aa_2"), swaps)


def low_lanes(shape):
    return lax.broadcasted_iota(jnp.int32, shape, len(shape) - 1) < 64


def rms_rows(x):
    return (x * lax.rsqrt(jnp.mean(x * x, axis=-1, keepdims=True) + EPSILON)).astype(BF16)


def matmul(a, b):
    return jnp.dot(a, b, preferred_element_type=F32)


def matmul_t(a, b):
    return lax.dot_general(a, b, (((1,), (1,)), ((), ())), preferred_element_type=F32)


def head_norm(x, gain):
    row = lax.broadcasted_iota(jnp.int32, (256, 256), 0) // 64
    col = lax.broadcasted_iota(jnp.int32, (256, 256), 1) // 64
    averager = jnp.where(row == col, 1.0 / 64, 0.0).astype(BF16)
    squares = (x * x).astype(BF16)
    means = [matmul(squares[:, at : at + 256], averager) for at in range(0, x.shape[1], 256)]
    return x * lax.rsqrt(jnp.concatenate(means, axis=1) + EPSILON) * gain


def pair_of(x, p):
    return x[:, 128 * p : 128 * (p + 1)]


def attend(q, k, v):
    low = low_lanes(q.shape)
    values_low = low_lanes(v.shape)
    zero, one = jnp.zeros_like(q), jnp.ones_like(v)
    even = jnp.exp2(matmul_t(jnp.where(low, q, zero), k)).astype(BF16)
    odd = jnp.exp2(matmul_t(jnp.where(low, zero, q), k)).astype(BF16)
    even = matmul(even, jnp.where(values_low, v, one))
    odd = matmul(odd, jnp.where(values_low, one, v))
    return jnp.where(low, even, odd), jnp.where(low, odd, even)


def attend_whole(q, k, v):
    numerator, crossed = attend(q, k, v)
    return (numerator / pltpu.roll(crossed, 64, axis=1)).astype(BF16)


def hand_out(blocks_ref, outs):
    mine = own_pair()
    for k, out in enumerate(outs):
        out[...] = blocks_ref[mine ^ k]


def swap(x):
    return pltpu.roll(x, 64, axis=1)


def key_value_heads(keys, values):
    out = []
    for p in range(PAIRS):
        k, v = pair_of(keys, p), pair_of(values, p)
        low = low_lanes(k.shape)
        out.append(jnp.where(low, k, swap(v)).astype(BF16))
        out.append(jnp.where(low, swap(k), v).astype(BF16))
    return out


def query_heads(queries):
    half = queries.shape[0] // 2
    out = []
    for p in range(PAIRS):
        q = pair_of(queries, p)
        s = swap(q)
        low = low_lanes((half, 128))
        out.append(jnp.where(low, q[:half], s[half:]).astype(BF16))
        out.append(jnp.where(low, s[:half], q[half:]).astype(BF16))
    return out


def with_ones(kv, low):
    return jnp.where(low, jnp.ones_like(kv), kv)


def project_kernel(
    tokens_hbm,
    latents_hbm,
    wq_hbm,
    wkv_hbm,
    gain_hbm,
    send_ref,
    tokens_ref,
    latents_ref,
    wq_ref,
    wkv_ref,
    gain_ref,
    sems,
):
    half = wkv_ref.shape[1] // 2
    copies = [
        pltpu.make_async_copy(src, dst, sems.at[i])
        for i, (src, dst) in enumerate(
            (
                (gain_hbm, gain_ref),
                (latents_hbm, latents_ref),
                (tokens_hbm, tokens_ref),
                (wq_hbm, wq_ref),
                (wkv_hbm.at[:, :half], wkv_ref.at[:, :half]),
                (wkv_hbm.at[:, half:], wkv_ref.at[:, half:]),
            )
        )
    ]
    for copy in copies:
        copy.start()
    groups = send_ref.shape[0] // HEADS
    count = tokens_ref.shape[0] // groups
    copies[0].wait()
    copies[1].wait()
    latents = rms_rows(latents_ref[...].astype(F32))
    copies[2].wait()
    normed = rms_rows(tokens_ref[...].astype(F32))
    copies[3].wait()
    queries = head_norm(matmul(latents, wq_ref[...]), gain_ref[0:1, :] * QUERY_SCALE)
    for h, block in enumerate(query_heads(queries)):
        for g in range(groups):
            send_ref[g * HEADS + h, count:, :] = block
    copies[4].wait()
    keys = head_norm(matmul(normed, wkv_ref[:, :half]), gain_ref[1:2, :])
    copies[5].wait()
    values = matmul(normed, wkv_ref[:, half:])
    for h, block in enumerate(key_value_heads(keys, values)):
        for g in range(groups):
            send_ref[g * HEADS + h, :count, :] = block[g * count : (g + 1) * count]


def write_query_kernel(tokens_ref, wwq_ref, gain_ref, o0, o1, o2, o3, blocks_ref):
    normed = rms_rows(tokens_ref[...].astype(F32))
    queries = head_norm(matmul(normed, wwq_ref[...]), gain_ref[4:5, :] * QUERY_SCALE).astype(BF16)
    for p in range(PAIRS):
        blocks_ref[p] = pair_of(queries, p)
    hand_out(blocks_ref, (o0, o1, o2, o3))


def read_kernel(got_ref, out_ref):
    devices, rows, _ = got_ref.shape
    count = rows - 16
    kv = got_ref[:, :count, :].reshape(devices * count, 128)
    kv1 = with_ones(kv, low_lanes(kv.shape))
    step = 8
    for at in range(0, devices, step):
        packed = got_ref[at : at + step, count:, :].reshape(step * 16, 128).astype(F32)
        low = low_lanes(packed.shape)
        q = jnp.concatenate([packed, swap(packed)], axis=0)
        q = jnp.where(low_lanes(q.shape), q, 0.0).astype(BF16)
        o = matmul(jnp.exp2(matmul_t(q, kv)).astype(BF16), kv1)
        top, bottom = o[: step * 16], o[step * 16 :]
        numerators = jnp.where(low, swap(top), bottom)
        out_ref[at : at + step, :16] = numerators.astype(BF16).reshape(step, 16, 128)
        denominators = jnp.where(low, top, swap(bottom)).reshape(step, 2, 8, 128)
        part = lax.broadcasted_iota(jnp.int32, (step, 8, 128), 2) // 32 % 2
        denominators = jnp.where(part == 0, denominators[:, 0], denominators[:, 1])
        out_ref[at : at + step, 16:] = denominators.astype(BF16)


def unpacked_heads(got_ref):
    groups = got_ref.shape[0] // HEADS
    first = lax.broadcasted_iota(jnp.int32, (8, 128), 1) // 32 % 2 == 0
    heads = []
    for h in range(HEADS):
        total = got_ref[h].astype(F32)
        for g in range(1, groups):
            total = total + got_ref[g * HEADS + h].astype(F32)
        numerators, packed = total[:16], total[16:]
        top, bottom = jnp.where(first, packed, 0.0), jnp.where(first, 0.0, packed)
        top = top + pltpu.roll(top, 32, axis=1)
        bottom = bottom + pltpu.roll(bottom, 96, axis=1)
        heads.append(numerators / jnp.concatenate([top, bottom], axis=0))
    return heads


def self_project_kernel(
    got_ref, latents_ref, wo_ref, wqkv_ref, gain_ref, rows_ref, send_ref, q0, q1, q2, q3, blocks_ref
):
    devices = got_ref.shape[0]
    count = latents_ref.shape[0]
    attended = []
    heads = unpacked_heads(got_ref)
    low = low_lanes(heads[0].shape)
    for e, o in zip(heads[0::2], heads[1::2]):
        top, bottom = jnp.where(low, e, swap(o)), jnp.where(low, swap(e), o)
        attended.append(jnp.concatenate([top, bottom], axis=0).astype(BF16))
    attended = jnp.concatenate(attended, axis=1)
    rows = (latents_ref[...].astype(F32) + matmul(attended, wo_ref[...])).astype(BF16)
    rows_ref[...] = rows
    triple = matmul(rms_rows(rows.astype(F32)), wqkv_ref[...])
    queries = head_norm(triple[:, :512], gain_ref[2:3, :] * QUERY_SCALE).astype(BF16)
    keys = head_norm(triple[:, 512:1024], gain_ref[3:4, :]).astype(BF16)
    values = triple[:, 1024:].astype(BF16)
    for p in range(PAIRS):
        blocks_ref[p] = pair_of(queries, p)
    for d in range(devices):
        send_ref[d, :count] = pair_of(keys, d % PAIRS)
        send_ref[d, count:] = pair_of(values, d % PAIRS)
    hand_out(blocks_ref, (q0, q1, q2, q3))


def keys_of(got_ref):
    devices, rows, _ = got_ref.shape
    return got_ref[:, : rows // 2].reshape(devices * rows // 2, 128)


def values_of(got_ref):
    devices, rows, _ = got_ref.shape
    return got_ref[:, rows // 2 :].reshape(devices * rows // 2, 128)


def attend_kernel(got_ref, *refs):
    queries, outs = refs[: len(refs) // 2], refs[len(refs) // 2 :]
    count = queries[0].shape[0]
    q = jnp.concatenate([q[...] for q in queries], axis=0)
    result = attend_whole(q, keys_of(got_ref), values_of(got_ref))
    for i, out in enumerate(outs):
        out[...] = result[i * count : (i + 1) * count]


def gathered(blocks_ref, parts):
    mine = own_pair()
    for k, part in enumerate(parts):
        blocks_ref[mine ^ k] = part[...]
    return jnp.concatenate([blocks_ref[p] for p in range(PAIRS)], axis=1)


def write_project_kernel(
    a3, a2, a1, a0, rows_ref, wo_ref, wkv_ref, gain_ref, latents_ref, send_ref, blocks_ref
):
    attended = gathered(blocks_ref, (a0, a1, a2, a3))
    rows = (rows_ref[...].astype(F32) + matmul(attended, wo_ref[...])).astype(BF16)
    latents_ref[...] = rows
    count = rows.shape[0]
    kv = matmul(rms_rows(rows.astype(F32)), wkv_ref[...])
    keys = head_norm(kv[:, :512], gain_ref[5:6, :]).astype(BF16)
    values = kv[:, 512:].astype(BF16)
    for d in range(send_ref.shape[0]):
        send_ref[d, :count] = pair_of(keys, d % PAIRS)
        send_ref[d, count:] = pair_of(values, d % PAIRS)


def finish_kernel(a0, a1, a2, a3, tokens_ref, wo_ref, out_ref, blocks_ref):
    update = matmul(gathered(blocks_ref, (a0, a1, a2, a3)), wo_ref[...])
    out_ref[...] = (tokens_ref[...].astype(F32) + update).astype(BF16)


def call(body, outs, *args, scratch=(), fetch=None):
    space = pltpu.HBM if fetch else pltpu.VMEM
    scratch = list(scratch)
    if fetch:
        scratch += [pltpu.VMEM(a.shape, a.dtype) for a in args]
        scratch.append(pltpu.SemaphoreType.DMA((len(args) + fetch,)))
        args = [pltpu.with_memory_space_constraint(a, space) for a in args]
    results = pl.pallas_call(
        body,
        out_shape=tuple(jax.ShapeDtypeStruct(s, BF16) for s in outs),
        in_specs=[pl.BlockSpec(memory_space=space)] * len(args),
        out_specs=tuple(pl.BlockSpec(memory_space=pltpu.VMEM) for _ in outs),
        scratch_shapes=scratch,
        compiler_params=pltpu.CompilerParams(vmem_limit_bytes=48 * 1024 * 1024),
        cost_estimate=pl.CostEstimate(
            flops=10**9,
            transcendentals=0,
            bytes_accessed=sum(a.size * a.dtype.itemsize for a in args),
        ),
    )(*args)
    return results if len(outs) > 1 else results[0]


def blocks(rows):
    return [pltpu.VMEM((PAIRS, rows, 128), BF16)]


def all_to_all(x):
    return lax.all_to_all(x, AA, split_axis=0, concat_axis=0, tiled=True)


def swapped(parts):
    return tuple(to_peer(parts[k], k) for k in (3, 2, 1)) + (parts[0],)


def layer(
    tokens,
    latents,
    read_query,
    read_keyval,
    read_out,
    self_qkv,
    self_out,
    write_query,
    write_keyval,
    write_out,
    qk_gain,
):
    count, rows = tokens.shape[0], latents.shape[0]
    devices = lax.axis_size(AA)
    sent = call(
        project_kernel,
        ((devices, count * HEADS // devices + 16, 128),),
        tokens,
        latents,
        read_query,
        read_keyval,
        qk_gain,
        fetch=1,
    )
    partial = call(read_kernel, ((devices, 24, 128),), all_to_all(sent))
    own_rows, sent, *queries = call(
        self_project_kernel,
        ((rows, 1024), (devices, 2 * rows, 128)) + ((rows, 128),) * 4,
        all_to_all(partial),
        latents,
        read_out,
        self_qkv,
        qk_gain,
        scratch=blocks(rows),
    )
    asked = call(
        write_query_kernel,
        ((count, 128),) * 4,
        tokens,
        write_query,
        qk_gain,
        scratch=blocks(count),
    )
    q3, q2, q1, q0 = swapped(asked)
    got = all_to_all(sent)
    queries = swapped(queries)
    attended = call(attend_kernel, ((rows, 128),) * 4, got, *queries)[::-1]
    latents_out, sent = call(
        write_project_kernel,
        ((rows, 1024), (devices, 2 * rows, 128)),
        *swapped(attended),
        own_rows,
        self_out,
        write_keyval,
        qk_gain,
        scratch=blocks(rows),
    )
    sent, q3, q2, q1, q0 = lax.optimization_barrier((sent, q3, q2, q1, q0))
    got = all_to_all(sent)
    a3, a2 = call(attend_kernel, ((count, 128),) * 2, got, q3, q2)
    a3, a2 = to_peer(a3, 3), to_peer(a2, 2)
    a1 = to_peer(call(attend_kernel, ((count, 128),), got, q1), 1)
    a0 = call(attend_kernel, ((count, 128),), got, q0)
    tokens_out = call(
        finish_kernel,
        ((count, 1024),),
        a0,
        a1,
        a2,
        a3,
        tokens,
        write_out,
        scratch=blocks(count),
    )
    return (tokens_out, latents_out)


def solution(mesh):
    torus = Mesh(mesh.devices.reshape(mesh.shape["ba"], 4, 4, 2), ("ba", "aa_0", "aa_1", "aa_2"))
    in_specs = (P(BA_AA, None), P(BA_AA, None), P(), P(), P(), P(), P(), P(), P(), P(), P())
    out_specs = (P(BA_AA, None), P(BA_AA, None))
    return jax.shard_map(layer, mesh=torus, in_specs=in_specs, out_specs=out_specs, check_vma=False)
```

profile of v0, /device:TPU:1, one launch (start us, length us, event | category | flops | bytes accessed | tf_op | source)
XLA Modules:
  0.0 85.8 jit_solution(7593189776128752138)
XLA Ops:
  0.6 2.9 %shard_map.122 = bf16[32,64,128]{2,1,0:T(8,128)(2,1)S(1)} custom-call(bf16[192,1024]{1,0:T(8,128)(2,1)} %tokens_ref.3, bf16[32,1024]{1,0:T(8,128)(2,1)} %latents_ref.1, bf16[1024,512]{1,0:T(8,128)(2,1)} %wq_hbm.1, bf16[1024,1024]{1,0:T(8,128)(2,1)} %wkv_hbm.1, f32[6,512]{1,0:T(8,128)} %gain_ref.5), custom_call_target="tpu_custom_call" | custom-call | flops 1000000000 | bytes 3616768 | tf_op jit(solution)/shard_map/pallas_call | solution.py:286
  3.6 0.0 copy-start.1
  3.6 20.1 %all_to_all.20.got_ref = bf16[32,64,128]{2,1,0:T(8,128)(2,1)S(1)} all-to-all(bf16[32,64,128]{2,1,0:T(8,128)(2,1)S(1)} %shard_map.122), channel_id=1, replica_groups=mesh['ba'=8,'aa_0'=4,'aa_1'=4,'aa_2'=2] {'aa_0','aa_1','aa_2'}, dimensions={0} | all-to-all | bytes 1048576 | tf_op jit(solution)/shard_map/all_to_all | solution.py:307
  23.7 0.0 copy-start
  23.7 0.0 copy-start.3
  23.7 0.0 copy-start.4
  23.7 1.9 %shard_map.123 = bf16[32,24,128]{2,1,0:T(8,128)(2,1)S(1)} custom-call(bf16[32,64,128]{2,1,0:T(8,128)(2,1)S(1)} %all_to_all.20.got_ref), custom_call_target="tpu_custom_call" | custom-call | flops 1000000000 | bytes 524288 | tf_op jit(solution)/shard_map/pallas_call | solution.py:286
  25.6 11.7 %all_to_all.21.got_ref = bf16[32,24,128]{2,1,0:T(8,128)(2,1)S(1)} all-to-all(bf16[32,24,128]{2,1,0:T(8,128)(2,1)S(1)} %shard_map.123), channel_id=1, replica_groups=mesh['ba'=8,'aa_0'=4,'aa_1'=4,'aa_2'=2] {'aa_0','aa_1','aa_2'}, dimensions={0} | all-to-all | bytes 393216 | tf_op jit(solution)/shard_map/all_to_all | solution.py:307
  37.3 0.0 copy-done.1
  37.3 0.0 copy-done
  37.3 0.0 copy-done.3
  37.3 0.0 copy-done.4
  37.3 2.1 %shard_map.124 = (bf16[32,1024]{1,0:T(8,128)(2,1)S(1)}, bf16[32,64,128]{2,1,0:T(8,128)(2,1)}, bf16[32,128]{1,0:T(8,128)(2,1)S(1)}, bf16[32,128]{1,0:T(8,128)(2,1...) custom-call(bf16[32,24,128]{2,1,0:T(8,128)(2,1)S(1)} %all_to_all.21.got_ref, ...), custom_call_target="tpu_custom_call" | custom-call | flops 1000000000 | bytes 4468736 | tf_op jit(solution)/shard_map/pallas_call | solution.py:286
  39.4 3.8 %all-to-all-start.2 = ((bf16[32,64,128]{2,1,0:T(8,128)(2,1)}), bf16[32,64,128]{2,1,0:T(8,128)(2,1)S(1)}, u32[]{:S(2)}, u32[]{:S(2)}) async-start(bf16[32,64,128]{2,1,0:T(8,128)(2,1)} %get-tuple-element.25), calls=%async_computation.2 | async-start | bytes 1048576 | tf_op jit(solution)/shard_map/all_to_all | solution.py:307
  43.2 0.0 copy-start.2
  43.3 0.0 copy-start.6
  43.3 1.7 %collective-permute-start = (bf16[32,128]{1,0:T(8,128)(2,1)S(1)}, bf16[32,128]{1,0:T(8,128)(2,1)S(1)}, u32[]{:S(2)}, u32[]{:S(2)}) collective-permute-start(bf16[32,128]{1,0:T(8,128)(2,1)S(1)} %get-tuple-element.26), channel_id=1, source_target_pairs={{0,3},{1,2},{2,1},{3,0},{4,7},{5,6},{6,5},{7,4},{8,11},{9,10},{10,... | collective-permute-start | bytes 24584 | tf_op jit(solution)/shard_map/ppermute | solution.py:27
  45.0 0.1 collective-permute-start.1
  45.1 0.4 collective-permute-start.2
  45.5 2.0 %collective-permute-done.refs_0_ = bf16[32,128]{1,0:T(8,128)(2,1)S(1)} collective-permute-done((bf16[32,128]{1,0:T(8,128)(2,1)S(1)}, bf16[32,128]{1,0:T(8,128)(2,1)S(1)}, u32[]{:S(2)}, u32[]{:S(2)}) %collective-permute-start) | collective-permute-done | bytes 8224 | tf_op jit(solution)/shard_map/ppermute | solution.py:27
  47.5 0.6 collective-permute-done.1.refs_1_
  48.1 0.0 collective-permute-done.2.refs_2_
  48.1 6.8 %all-to-all-done.2.got_ref = bf16[32,64,128]{2,1,0:T(8,128)(2,1)S(1)} async-done(((bf16[32,64,128]{2,1,0:T(8,128)(2,1)}), bf16[32,64,128]{2,1,0:T(8,128)(2,1)S(1)}, u32[]{:S(2)}, u32[]{:S(2)}) %all-to-all-start.2) | async-done | bytes 524320 | tf_op jit(solution)/shard_map/all_to_all | solution.py:307
  55.0 0.5 shard_map.125
  55.5 0.0 copy-start.5
  55.5 0.0 copy-start.7
  55.5 0.1 collective-permute-start.3
  55.6 1.0 %collective-permute-start.4 = (bf16[32,128]{1,0:T(8,128)(2,1)S(1)}, bf16[32,128]{1,0:T(8,128)(2,1)S(1)}, u32[]{:S(2)}, u32[]{:S(2)}) collective-permute-start(bf16[32,128]{1,0:T(8,128)(2,1)S(1)} %get-tuple-element.31), channel_id=1, source_target_pairs={{0,2},{1,3},{2,0},{3,1},{4,6},{5,7},{6,4},{7,5},{8,10},{9,11},{10,... | collective-permute-start | bytes 24584 | tf_op jit(solution)/shard_map/ppermute | solution.py:27
  56.6 1.1 %collective-permute-start.5 = (bf16[32,128]{1,0:T(8,128)(2,1)S(1)}, bf16[32,128]{1,0:T(8,128)(2,1)S(1)}, u32[]{:S(2)}, u32[]{:S(2)}) collective-permute-start(bf16[32,128]{1,0:T(8,128)(2,1)S(1)} %get-tuple-element.32), channel_id=1, source_target_pairs={{0,1},{1,0},{2,3},{3,2},{4,5},{5,4},{6,7},{7,6},{8,9},{9,8},{10,11... | collective-permute-start | bytes 24584 | tf_op jit(solution)/shard_map/ppermute | solution.py:27
  57.7 0.0 copy-done.2
  57.7 0.0 copy-done.6
  57.7 0.6 shard_map.127
  58.4 0.1 collective-permute-start.6
  58.5 1.3 %collective-permute-start.7 = (bf16[192,128]{1,0:T(8,128)(2,1)S(1)}, bf16[192,128]{1,0:T(8,128)(2,1)S(1)}, u32[]{:S(2)}, u32[]{:S(2)}) collective-permute-start(bf16[192,128]{1,0:T(8,128)(2,1)S(1)} %get-tuple-element.37), channel_id=1, source_target_pairs={{0,2},{1,3},{2,0},{3,1},{4,6},{5,7},{6,4},{7,5},{8,10},{9,11},{10,... | collective-permute-start | bytes 147464 | tf_op jit(solution)/shard_map/ppermute | solution.py:27
  59.8 0.0 collective-permute-done.3.a3
  59.8 0.8 collective-permute-start.8
  60.6 0.0 collective-permute-done.4.a2
  60.6 0.0 collective-permute-done.5.a1
  60.6 0.0 copy-done.5
  60.6 0.0 copy-done.7
  60.6 1.3 %shard_map.126 = (bf16[32,1024]{1,0:T(8,128)(2,1)}, bf16[32,64,128]{2,1,0:T(8,128)(2,1)S(1)}) custom-call(bf16[32,128]{1,0:T(8,128)(2,1)S(1)} %collective-permute-done.3.a3, bf16[32,128]{1,0:T(8,128)(2,1)S(1)} %collective-permute-done.4.a2, bf16[32,128]{1,0:T(8,128)(2,1)S(1)} %collective-permute-done.5.a1, bf16[32,128]{1,0:T(8,128)(2,1)S(1)} %get-tuple-element.33.a0, ...), custom_call_target="tpu_custom_call" | custom-call | flops 1000000000 | bytes 3256320 | tf_op jit(solution)/shard_map/pallas_call | solution.py:286
  62.0 0.4 collective-permute-done.6.refs_0_
  62.3 0.0 collective-permute-done.7.refs_1_
  62.4 0.0 collective-permute-done.8.refs_0_
  62.4 16.5 %all_to_all.22.got_ref = bf16[32,64,128]{2,1,0:T(8,128)(2,1)S(1)} all-to-all(bf16[32,64,128]{2,1,0:T(8,128)(2,1)S(1)} %get-tuple-element.40), channel_id=1, replica_groups=mesh['ba'=8,'aa_0'=4,'aa_1'=4,'aa_2'=2] {'aa_0','aa_1','aa_2'}, dimensions={0} | all-to-all | bytes 1048576 | tf_op jit(solution)/shard_map/all_to_all | solution.py:307
  78.8 1.0 %shard_map.130 = (bf16[192,128]{1,0:T(8,128)(2,1)S(1)}, bf16[192,128]{1,0:T(8,128)(2,1)S(1)}) custom-call(bf16[32,64,128]{2,1,0:T(8,128)(2,1)S(1)} %all_to_all.22.got_ref, bf16[192,128]{1,0:T(8,128)(2,1)S(1)} %collective-permute-done.6.refs_0_, bf16[192,128]{1,0:T(8,128)(2,1)S(1)} %collective-permute-done.7.refs_1_), custom_call_target="tpu_custom_call" | custom-call | flops 1000000000 | bytes 622592 | tf_op jit(solution)/shard_map/pallas_call | solution.py:286
  79.9 0.2 collective-permute-start.10
  80.1 1.2 %collective-permute-start.11 = (bf16[192,128]{1,0:T(8,128)(2,1)S(1)}, bf16[192,128]{1,0:T(8,128)(2,1)S(1)}, u32[]{:S(2)}, u32[]{:S(2)}) collective-permute-start(bf16[192,128]{1,0:T(8,128)(2,1)S(1)} %get-tuple-element.46), channel_id=1, source_target_pairs={{0,3},{1,2},{2,1},{3,0},{4,7},{5,6},{6,5},{7,4},{8,11},{9,10},{10,... | collective-permute-start | bytes 147464 | tf_op jit(solution)/shard_map/ppermute | solution.py:27
  81.3 0.7 shard_map.129
  82.0 0.0 copy-start.8
  82.0 0.6 collective-permute-start.9
  82.6 0.7 shard_map.128.a0
  83.3 0.3 collective-permute-done.10.a2
  83.6 1.1 %collective-permute-done.11.a3 = bf16[192,128]{1,0:T(8,128)(2,1)S(1)} collective-permute-done((bf16[192,128]{1,0:T(8,128)(2,1)S(1)}, bf16[192,128]{1,0:T(8,128)(2,1)S(1)}, u32[]{:S(2)}, u32[]{:S(2)}) %collective-permute-start.11) | collective-permute-done | bytes 49184 | tf_op jit(solution)/shard_map/ppermute | solution.py:27
  84.6 0.0 collective-permute-done.9.a1
  84.6 0.0 copy-done.8
  84.6 1.1 %shard_map.131 = bf16[192,1024]{1,0:T(8,128)(2,1)} custom-call(bf16[192,128]{1,0:T(8,128)(2,1)S(1)} %shard_map.128.a0, bf16[192,128]{1,0:T(8,128)(2,1)S(1)} %collective-permute-done.9.a1, bf16[192,128]{1,0:T(8,128)(2,1)S(1)} %collective-permute-done.10.a2, bf16[192,128]{1,0:T(8,128)(2,1)S(1)} %collective-permute-done.11.a3, bf16[192,1024]{1,0:T(8,128)(2,1)S(1)} %copy-done.2, ...), custom_call_target="tpu_custom_call" | custom-call | flops 1000000000 | bytes 1638400 | tf_op jit(solution)/shard_map/pallas_call | solution.py:286
Async XLA Ops:
  3.6 33.7 %copy-start.1 = (bf16[512,1024]{1,0:T(8,128)(2,1)S(1)}, bf16[512,1024]{1,0:T(8,128)(2,1)}, u32[]{:S(2)}) copy-start(bf16[512,1024]{1,0:T(8,128)(2,1)} %wo_ref.3) | copy-start | bytes 3145732
  23.7 13.6 %copy-start = (bf16[1024,1536]{1,0:T(8,128)(2,1)S(1)}, bf16[1024,1536]{1,0:T(8,128)(2,1)}, u32[]{:S(2)}) copy-start(bf16[1024,1536]{1,0:T(8,128)(2,1)} %wqkv_ref.1) | copy-start | bytes 9437188
  23.7 13.6 %copy-start.3 = (bf16[32,1024]{1,0:T(8,128)(2,1)S(1)}, bf16[32,1024]{1,0:T(8,128)(2,1)}, u32[]{:S(2)}) copy-start(bf16[32,1024]{1,0:T(8,128)(2,1)} %latents_ref.1) | copy-start | bytes 196612
  23.7 13.6 %copy-start.4 = (f32[6,512]{1,0:T(8,128)S(1)}, f32[6,512]{1,0:T(8,128)}, u32[]{:S(2)}) copy-start(f32[6,512]{1,0:T(8,128)} %gain_ref.5) | copy-start | bytes 36868
  39.4 15.6 %all-to-all-start.2 = ((bf16[32,64,128]{2,1,0:T(8,128)(2,1)}), bf16[32,64,128]{2,1,0:T(8,128)(2,1)S(1)}, u32[]{:S(2)}, u32[]{:S(2)}) async-start(bf16[32,64,128]{2,1,0:T(8,128)(2,1)} %get-tuple-element.25), calls=%async_computation.2 | async-start | bytes 1048576 | tf_op jit(solution)/shard_map/all_to_all | solution.py:307
  43.2 14.5 %copy-start.2 = (bf16[192,1024]{1,0:T(8,128)(2,1)S(1)}, bf16[192,1024]{1,0:T(8,128)(2,1)}, u32[]{:S(2)}) copy-start(bf16[192,1024]{1,0:T(8,128)(2,1)} %tokens_ref.3) | copy-start | bytes 1179652
  43.3 14.5 %copy-start.6 = (bf16[1024,512]{1,0:T(8,128)(2,1)S(1)}, bf16[1024,512]{1,0:T(8,128)(2,1)}, u32[]{:S(2)}) copy-start(bf16[1024,512]{1,0:T(8,128)(2,1)} %wwq_ref.1) | copy-start | bytes 3145732
  43.3 4.3 %collective-permute-start = (bf16[32,128]{1,0:T(8,128)(2,1)S(1)}, bf16[32,128]{1,0:T(8,128)(2,1)S(1)}, u32[]{:S(2)}, u32[]{:S(2)}) collective-permute-start(bf16[32,128]{1,0:T(8,128)(2,1)S(1)} %get-tuple-element.26), channel_id=1, source_target_pairs={{0,3},{1,2},{2,1},{3,0},{4,7},{5,6},{6,5},{7,4},{8,11},{9,10},{10,... | collective-permute-start | bytes 24584 | tf_op jit(solution)/shard_map/ppermute | solution.py:27
  45.0 3.1 %collective-permute-start.1 = (bf16[32,128]{1,0:T(8,128)(2,1)S(1)}, bf16[32,128]{1,0:T(8,128)(2,1)S(1)}, u32[]{:S(2)}, u32[]{:S(2)}) collective-permute-start(bf16[32,128]{1,0:T(8,128)(2,1)S(1)} %get-tuple-element.27), channel_id=1, source_target_pairs={{0,2},{1,3},{2,0},{3,1},{4,6},{5,7},{6,4},{7,5},{8,10},{9,11},{10,... | collective-permute-start | bytes 24584 | tf_op jit(solution)/shard_map/ppermute | solution.py:27
  45.1 3.1 %collective-permute-start.2 = (bf16[32,128]{1,0:T(8,128)(2,1)S(1)}, bf16[32,128]{1,0:T(8,128)(2,1)S(1)}, u32[]{:S(2)}, u32[]{:S(2)}) collective-permute-start(bf16[32,128]{1,0:T(8,128)(2,1)S(1)} %get-tuple-element.28), channel_id=1, source_target_pairs={{0,1},{1,0},{2,3},{3,2},{4,5},{5,4},{6,7},{7,6},{8,9},{9,8},{10,11... | collective-permute-start | bytes 24584 | tf_op jit(solution)/shard_map/ppermute | solution.py:27
  55.5 5.1 %copy-start.5 = (bf16[1024,1024]{1,0:T(8,128)(2,1)S(1)}, bf16[1024,1024]{1,0:T(8,128)(2,1)}, u32[]{:S(2)}) copy-start(bf16[1024,1024]{1,0:T(8,128)(2,1)} %wkv_ref.1) | copy-start | bytes 6291460
  55.5 5.1 %copy-start.7 = (bf16[512,1024]{1,0:T(8,128)(2,1)S(1)}, bf16[512,1024]{1,0:T(8,128)(2,1)}, u32[]{:S(2)}) copy-start(bf16[512,1024]{1,0:T(8,128)(2,1)} %wo_ref.4) | copy-start | bytes 3145732
  55.5 4.3 %collective-permute-start.3 = (bf16[32,128]{1,0:T(8,128)(2,1)S(1)}, bf16[32,128]{1,0:T(8,128)(2,1)S(1)}, u32[]{:S(2)}, u32[]{:S(2)}) collective-permute-start(bf16[32,128]{1,0:T(8,128)(2,1)S(1)} %get-tuple-element.30), channel_id=1, source_target_pairs={{0,3},{1,2},{2,1},{3,0},{4,7},{5,6},{6,5},{7,4},{8,11},{9,10},{10,... | collective-permute-start | bytes 24584 | tf_op jit(solution)/shard_map/ppermute | solution.py:27
  55.6 5.0 %collective-permute-start.4 = (bf16[32,128]{1,0:T(8,128)(2,1)S(1)}, bf16[32,128]{1,0:T(8,128)(2,1)S(1)}, u32[]{:S(2)}, u32[]{:S(2)}) collective-permute-start(bf16[32,128]{1,0:T(8,128)(2,1)S(1)} %get-tuple-element.31), channel_id=1, source_target_pairs={{0,2},{1,3},{2,0},{3,1},{4,6},{5,7},{6,4},{7,5},{8,10},{9,11},{10,... | collective-permute-start | bytes 24584 | tf_op jit(solution)/shard_map/ppermute | solution.py:27
  56.6 4.0 %collective-permute-start.5 = (bf16[32,128]{1,0:T(8,128)(2,1)S(1)}, bf16[32,128]{1,0:T(8,128)(2,1)S(1)}, u32[]{:S(2)}, u32[]{:S(2)}) collective-permute-start(bf16[32,128]{1,0:T(8,128)(2,1)S(1)} %get-tuple-element.32), channel_id=1, source_target_pairs={{0,1},{1,0},{2,3},{3,2},{4,5},{5,4},{6,7},{7,6},{8,9},{9,8},{10,11... | collective-permute-start | bytes 24584 | tf_op jit(solution)/shard_map/ppermute | solution.py:27
  58.4 4.0 %collective-permute-start.6 = (bf16[192,128]{1,0:T(8,128)(2,1)S(1)}, bf16[192,128]{1,0:T(8,128)(2,1)S(1)}, u32[]{:S(2)}, u32[]{:S(2)}) collective-permute-start(bf16[192,128]{1,0:T(8,128)(2,1)S(1)} %get-tuple-element.36), channel_id=1, source_target_pairs={{0,3},{1,2},{2,1},{3,0},{4,7},{5,6},{6,5},{7,4},{8,11},{9,10},{10,... | collective-permute-start | bytes 147464 | tf_op jit(solution)/shard_map/ppermute | solution.py:27
  58.5 3.9 %collective-permute-start.7 = (bf16[192,128]{1,0:T(8,128)(2,1)S(1)}, bf16[192,128]{1,0:T(8,128)(2,1)S(1)}, u32[]{:S(2)}, u32[]{:S(2)}) collective-permute-start(bf16[192,128]{1,0:T(8,128)(2,1)S(1)} %get-tuple-element.37), channel_id=1, source_target_pairs={{0,2},{1,3},{2,0},{3,1},{4,6},{5,7},{6,4},{7,5},{8,10},{9,11},{10,... | collective-permute-start | bytes 147464 | tf_op jit(solution)/shard_map/ppermute | solution.py:27
  59.8 2.5 %collective-permute-start.8 = (bf16[192,128]{1,0:T(8,128)(2,1)S(1)}, bf16[192,128]{1,0:T(8,128)(2,1)S(1)}, u32[]{:S(2)}, u32[]{:S(2)}) collective-permute-start(bf16[192,128]{1,0:T(8,128)(2,1)S(1)} %get-tuple-element.38), channel_id=1, source_target_pairs={{0,1},{1,0},{2,3},{3,2},{4,5},{5,4},{6,7},{7,6},{8,9},{9,8},{10,11... | collective-permute-start | bytes 147464 | tf_op jit(solution)/shard_map/ppermute | solution.py:27
  79.9 3.7 %collective-permute-start.10 = (bf16[192,128]{1,0:T(8,128)(2,1)S(1)}, bf16[192,128]{1,0:T(8,128)(2,1)S(1)}, u32[]{:S(2)}, u32[]{:S(2)}) collective-permute-start(bf16[192,128]{1,0:T(8,128)(2,1)S(1)} %get-tuple-element.45), channel_id=1, source_target_pairs={{0,2},{1,3},{2,0},{3,1},{4,6},{5,7},{6,4},{7,5},{8,10},{9,11},{10,... | collective-permute-start | bytes 147464 | tf_op jit(solution)/shard_map/ppermute | solution.py:27
  80.1 4.5 %collective-permute-start.11 = (bf16[192,128]{1,0:T(8,128)(2,1)S(1)}, bf16[192,128]{1,0:T(8,128)(2,1)S(1)}, u32[]{:S(2)}, u32[]{:S(2)}) collective-permute-start(bf16[192,128]{1,0:T(8,128)(2,1)S(1)} %get-tuple-element.46), channel_id=1, source_target_pairs={{0,3},{1,2},{2,1},{3,0},{4,7},{5,6},{6,5},{7,4},{8,11},{9,10},{10,... | collective-permute-start | bytes 147464 | tf_op jit(solution)/shard_map/ppermute | solution.py:27
  82.0 2.6 %copy-start.8 = (bf16[512,1024]{1,0:T(8,128)(2,1)S(1)}, bf16[512,1024]{1,0:T(8,128)(2,1)}, u32[]{:S(2)}) copy-start(bf16[512,1024]{1,0:T(8,128)(2,1)} %wo_ref.5) | copy-start | bytes 3145732
  82.0 2.6 %collective-permute-start.9 = (bf16[192,128]{1,0:T(8,128)(2,1)S(1)}, bf16[192,128]{1,0:T(8,128)(2,1)S(1)}, u32[]{:S(2)}, u32[]{:S(2)}) collective-permute-start(bf16[192,128]{1,0:T(8,128)(2,1)S(1)} %shard_map.129), channel_id=1, source_target_pairs={{0,1},{1,0},{2,3},{3,2},{4,5},{5,4},{6,7},{7,6},{8,9},{9,8},{10,11... | collective-permute-start | bytes 147464 | tf_op jit(solution)/shard_map/ppermute | solution.py:27
where the time goes:
time: 86.2 us; the launch traced here: 85.8 us
  blocking collectives  48.3 us (56%)
  Pallas kernels  12.9 us (15%)
  starting transfers between devices  12.6 us (15%)
  waiting for transfers between devices  11.2 us (13%)
    all_to_all x3, blocking collectives, all_to_all(): return lax.all_to_all(x, AA, split_axis=0, concat_axis=0, tiled=True)  48.3 us
    pallas_call x10, Pallas kernels, call(): pl.pallas_call(body, out_shape=tuple((jax.ShapeDtypeStruct(s, BF16) for s...  12.9 us
    ppermute x12, starting transfers between devices, to_peer(): return lax.ppermute(x, ('aa_1', 'aa_2'), swaps)  8.72 us
    all_to_all x1, waiting for transfers between devices, all_to_all(): return lax.all_to_all(x, AA, split_axis=0, concat_axis=0, tiled=True)  6.8 us
    ppermute x12, waiting for transfers between devices, to_peer(): return lax.ppermute(x, ('aa_1', 'aa_2'), swaps)  4.37 us
    all_to_all x1, starting transfers between devices, all_to_all(): return lax.all_to_all(x, AA, split_axis=0, concat_axis=0, tiled=True)  3.84 us
  transfers between devices with their start and end apart: 13, of which 6 were waited for; matrix products, arithmetic and copies ran while one was open for 0% of the time, Pallas kernels for 4%

commit v1 on v0

--- a/solution.py
+++ b/solution.py
@@ -205,7 +205,7 @@
 
 
 def self_project_kernel(
-    got_ref, latents_ref, wo_ref, wqkv_ref, gain_ref, rows_ref, send_ref, q0, q1, q2, q3, blocks_ref
+    got_ref, latents_ref, wo_ref, wqkv_ref, gain_ref, rows_ref, send_ref
 ):
     devices = got_ref.shape[0]
     count = latents_ref.shape[0]
@@ -218,16 +218,21 @@
     attended = jnp.concatenate(attended, axis=1)
     rows = (latents_ref[...].astype(F32) + matmul(attended, wo_ref[...])).astype(BF16)
     rows_ref[...] = rows
-    triple = matmul(rms_rows(rows.astype(F32)), wqkv_ref[...])
-    queries = head_norm(triple[:, :512], gain_ref[2:3, :] * QUERY_SCALE).astype(BF16)
-    keys = head_norm(triple[:, 512:1024], gain_ref[3:4, :]).astype(BF16)
-    values = triple[:, 1024:].astype(BF16)
-    for p in range(PAIRS):
-        blocks_ref[p] = pair_of(queries, p)
+    pairs = matmul(rms_rows(rows.astype(F32)), wqkv_ref[:, 512:])
+    keys = head_norm(pairs[:, :512], gain_ref[3:4, :]).astype(BF16)
+    values = pairs[:, 512:].astype(BF16)
     for d in range(devices):
         send_ref[d, :count] = pair_of(keys, d % PAIRS)
         send_ref[d, count:] = pair_of(values, d % PAIRS)
-    hand_out(blocks_ref, (q0, q1, q2, q3))
+
+
+def self_query_kernel(rows_ref, wqkv_ref, gain_ref, o0, o1, o2, o3, blocks_ref):
+    normed = rms_rows(rows_ref[...].astype(F32))
+    queries = matmul(normed, wqkv_ref[:, :512])
+    queries = head_norm(queries, gain_ref[2:3, :] * QUERY_SCALE).astype(BF16)
+    for p in range(PAIRS):
+        blocks_ref[p] = pair_of(queries, p)
+    hand_out(blocks_ref, (o0, o1, o2, o3))
 
 
 def keys_of(got_ref):
@@ -337,12 +342,19 @@
         fetch=1,
     )
     partial = call(read_kernel, ((devices, 24, 128),), all_to_all(sent))
-    own_rows, sent, *queries = call(
+    own_rows, sent = call(
         self_project_kernel,
-        ((rows, 1024), (devices, 2 * rows, 128)) + ((rows, 128),) * 4,
+        ((rows, 1024), (devices, 2 * rows, 128)),
         all_to_all(partial),
         latents,
         read_out,
+        self_qkv,
+        qk_gain,
+    )
+    queries = call(
+        self_query_kernel,
+        ((rows, 128),) * 4,
+        own_rows,
         self_qkv,
         qk_gain,
         scratch=blocks(rows),

time: 86.2 us -> 89 us (1.032)
  local copies, waits for them, and re-layouts: 0.05 us -> 2.07 us
    unnamed x18 -> x20, local copies, waits for them, and re-layouts: 0.05 us -> 2.07 us
    pallas_call x10 -> x11, Pallas kernels: 12.9 us -> 13.5 us  [call(): pl.pallas_call(body, out_shape=tuple((jax.ShapeDtypeStruct(s, BF16) for s...]
where the time goes in v1:
time: 89 us; the launch traced here: 88.6 us
  blocking collectives  48.3 us (54%)
  Pallas kernels  13.5 us (15%)
  starting transfers between devices  13.2 us (15%)
  waiting for transfers between devices  10.7 us (12%)
  local copies, waits for them, and re-layouts  2.07 us (2%)
    all_to_all x3, blocking collectives, all_to_all(): return lax.all_to_all(x, AA, split_axis=0, concat_axis=0, tiled=True)  48.3 us
    pallas_call x11, Pallas kernels, call(): pl.pallas_call(body, out_shape=tuple((jax.ShapeDtypeStruct(s, BF16) for s...  13.5 us
    ppermute x12, starting transfers between devices, to_peer(): return lax.ppermute(x, ('aa_1', 'aa_2'), swaps)  8.7 us
    all_to_all x1, waiting for transfers between devices, all_to_all(): return lax.all_to_all(x, AA, split_axis=0, concat_axis=0, tiled=True)  6.29 us
    all_to_all x1, starting transfers between devices, all_to_all(): return lax.all_to_all(x, AA, split_axis=0, concat_axis=0, tiled=True)  4.49 us
    ppermute x12, waiting for transfers between devices, to_peer(): return lax.ppermute(x, ('aa_1', 'aa_2'), swaps)  4.45 us
    unnamed x20, local copies, waits for them, and re-layouts  2.07 us
  transfers between devices with their start and end apart: 13, of which 6 were waited for; matrix products, arithmetic and copies ran while one was open for 0% of the time, Pallas kernels for 4%

profile of v1, /device:TPU:1, one launch (start us, length us, event | category | flops | bytes accessed | tf_op | source)
XLA Modules:
  0.0 88.6 jit_solution(17601904658863478395)
XLA Ops:
  0.6 2.9 %shard_map.122 = bf16[32,64,128]{2,1,0:T(8,128)(2,1)S(1)} custom-call(bf16[192,1024]{1,0:T(8,128)(2,1)} %tokens_ref.3, bf16[32,1024]{1,0:T(8,128)(2,1)} %latents_ref.1, bf16[1024,512]{1,0:T(8,128)(2,1)} %wq_hbm.1, bf16[1024,1024]{1,0:T(8,128)(2,1)} %wkv_hbm.1, f32[6,512]{1,0:T(8,128)} %gain_ref.7), custom_call_target="tpu_custom_call" | custom-call | flops 1000000000 | bytes 3616768 | tf_op jit(solution)/shard_map/pallas_call | solution.py:291
  3.6 0.0 copy-start.1
  3.6 20.1 %all_to_all.20.got_ref = bf16[32,64,128]{2,1,0:T(8,128)(2,1)S(1)} all-to-all(bf16[32,64,128]{2,1,0:T(8,128)(2,1)S(1)} %shard_map.122), channel_id=1, replica_groups=mesh['ba'=8,'aa_0'=4,'aa_1'=4,'aa_2'=2] {'aa_0','aa_1','aa_2'}, dimensions={0} | all-to-all | bytes 1048576 | tf_op jit(solution)/shard_map/all_to_all | solution.py:312
  23.7 0.0 copy-start
  23.7 0.0 copy-start.4
  23.7 0.0 copy-start.5
  23.7 1.9 %shard_map.123 = bf16[32,24,128]{2,1,0:T(8,128)(2,1)S(1)} custom-call(bf16[32,64,128]{2,1,0:T(8,128)(2,1)S(1)} %all_to_all.20.got_ref), custom_call_target="tpu_custom_call" | custom-call | flops 1000000000 | bytes 524288 | tf_op jit(solution)/shard_map/pallas_call | solution.py:291
  25.6 11.7 %all_to_all.21.got_ref = bf16[32,24,128]{2,1,0:T(8,128)(2,1)S(1)} all-to-all(bf16[32,24,128]{2,1,0:T(8,128)(2,1)S(1)} %shard_map.123), channel_id=1, replica_groups=mesh['ba'=8,'aa_0'=4,'aa_1'=4,'aa_2'=2] {'aa_0','aa_1','aa_2'}, dimensions={0} | all-to-all | bytes 393216 | tf_op jit(solution)/shard_map/all_to_all | solution.py:312
  37.3 0.0 copy-done.1
  37.3 0.0 copy-done
  37.3 0.0 copy-done.4
  37.3 0.0 copy-done.5
  37.3 1.0 %shard_map.124 = (bf16[32,1024]{1,0:T(8,128)(2,1)S(1)}, bf16[32,64,128]{2,1,0:T(8,128)(2,1)S(1)}) custom-call(bf16[32,24,128]{2,1,0:T(8,128)(2,1)S(1)} %all_to_all.21.got_ref, bf16[32,1024]{1,0:T(8,128)(2,1)S(1)} %copy-done.4, bf16[512,1024]{1,0:T(8,128)(2,1)S(1)} %copy-done.1, bf16[1024,1536]{1,0:T(8,128)(2,1)S(1)} %copy-done, f32[6,512]{1,0:T(8,128)S(1)} %copy-done.5), custom_call_target="tpu_custom_call" | custom-call | flops 1000000000 | bytes 4468736 | tf_op jit(solution)/shard_map/pallas_call | solution.py:291
  38.4 0.0 copy-start.2
  38.4 0.8 copy-done.2
  39.2 4.5 %all-to-all-start.2 = ((bf16[32,64,128]{2,1,0:T(8,128)(2,1)}), bf16[32,64,128]{2,1,0:T(8,128)(2,1)}, u32[]{:S(2)}, u32[]{:S(2)}) async-start(bf16[32,64,128]{2,1,0:T(8,128)(2,1)} %copy-done.2), calls=%async_computation.2 | async-start | bytes 1048576 | tf_op jit(solution)/shard_map/all_to_all | solution.py:312
  43.7 0.5 shard_map.125
  44.2 0.0 copy-start.3
  44.2 1.7 %collective-permute-start = (bf16[32,128]{1,0:T(8,128)(2,1)S(1)}, bf16[32,128]{1,0:T(8,128)(2,1)S(1)}, u32[]{:S(2)}, u32[]{:S(2)}) collective-permute-start(bf16[32,128]{1,0:T(8,128)(2,1)S(1)} %get-tuple-element.27), channel_id=1, source_target_pairs={{0,3},{1,2},{2,1},{3,0},{4,7},{5,6},{6,5},{7,4},{8,11},{9,10},{10,... | collective-permute-start | bytes 24584 | tf_op jit(solution)/shard_map/ppermute | solution.py:27
  45.9 0.1 collective-permute-start.1
  46.0 0.4 collective-permute-start.2
  46.4 1.6 %collective-permute-done.refs_0_ = bf16[32,128]{1,0:T(8,128)(2,1)S(1)} collective-permute-done((bf16[32,128]{1,0:T(8,128)(2,1)S(1)}, bf16[32,128]{1,0:T(8,128)(2,1)S(1)}, u32[]{:S(2)}, u32[]{:S(2)}) %collective-permute-start) | collective-permute-done | bytes 8224 | tf_op jit(solution)/shard_map/ppermute | solution.py:27
  48.0 1.1 %collective-permute-done.1.refs_1_ = bf16[32,128]{1,0:T(8,128)(2,1)S(1)} collective-permute-done((bf16[32,128]{1,0:T(8,128)(2,1)S(1)}, bf16[32,128]{1,0:T(8,128)(2,1)S(1)}, u32[]{:S(2)}, u32[]{:S(2)}) %collective-permute-start.1) | collective-permute-done | bytes 8224 | tf_op jit(solution)/shard_map/ppermute | solution.py:27
  49.1 0.0 collective-permute-done.2.refs_2_
  49.1 6.3 %all-to-all-done.2.got_ref = bf16[32,64,128]{2,1,0:T(8,128)(2,1)} async-done(((bf16[32,64,128]{2,1,0:T(8,128)(2,1)}), bf16[32,64,128]{2,1,0:T(8,128)(2,1)}, u32[]{:S(2)}, u32[]{:S(2)}) %all-to-all-start.2) | async-done | bytes 524320 | tf_op jit(solution)/shard_map/all_to_all | solution.py:312
  55.4 0.0 copy-start.8
  55.4 1.6 %shard_map.126 = (bf16[32,128]{1,0:T(8,128)(2,1)S(1)}, bf16[32,128]{1,0:T(8,128)(2,1)S(1)}, bf16[32,128]{1,0:T(8,128)(2,1)S(1)}, bf16[32,128]{1,0:T(8,128)(2,1)S(1)}) custom-call(bf16[32,64,128]{2,1,0:T(8,128)(2,1)} %all-to-all-done.2.got_ref, bf16[32,128]{1,0:T(8,128)(2,1)S(1)} %collective-permute-done.refs_0_, ...), custom_call_target="tpu_custom_call" | custom-call | flops 1000000000 | bytes 557056 | tf_op jit(solution)/shard_map/pallas_call | solution.py:291
  57.1 0.0 copy-start.6
  57.1 0.1 collective-permute-start.3
  57.2 1.0 %collective-permute-start.4 = (bf16[32,128]{1,0:T(8,128)(2,1)S(1)}, bf16[32,128]{1,0:T(8,128)(2,1)S(1)}, u32[]{:S(2)}, u32[]{:S(2)}) collective-permute-start(bf16[32,128]{1,0:T(8,128)(2,1)S(1)} %get-tuple-element.32), channel_id=1, source_target_pairs={{0,2},{1,3},{2,0},{3,1},{4,6},{5,7},{6,4},{7,5},{8,10},{9,11},{10,... | collective-permute-start | bytes 24584 | tf_op jit(solution)/shard_map/ppermute | solution.py:27
  58.2 1.1 %collective-permute-start.5 = (bf16[32,128]{1,0:T(8,128)(2,1)S(1)}, bf16[32,128]{1,0:T(8,128)(2,1)S(1)}, u32[]{:S(2)}, u32[]{:S(2)}) collective-permute-start(bf16[32,128]{1,0:T(8,128)(2,1)S(1)} %get-tuple-element.33), channel_id=1, source_target_pairs={{0,1},{1,0},{2,3},{3,2},{4,5},{5,4},{6,7},{7,6},{8,9},{9,8},{10,11... | collective-permute-start | bytes 24584 | tf_op jit(solution)/shard_map/ppermute | solution.py:27
  59.3 0.0 copy-done.3
  59.3 0.0 copy-start.7
  59.3 1.2 %copy-done.7 = bf16[1024,512]{1,0:T(8,128)(2,1)S(1)} copy-done((bf16[1024,512]{1,0:T(8,128)(2,1)S(1)}, bf16[1024,512]{1,0:T(8,128)(2,1)}, u32[]{:S(2)}) %copy-start.7) | copy-done | bytes 1048600
  60.6 0.6 shard_map.128
  61.2 0.1 collective-permute-start.6
  61.3 1.3 %collective-permute-start.7 = (bf16[192,128]{1,0:T(8,128)(2,1)S(1)}, bf16[192,128]{1,0:T(8,128)(2,1)S(1)}, u32[]{:S(2)}, u32[]{:S(2)}) collective-permute-start(bf16[192,128]{1,0:T(8,128)(2,1)S(1)} %get-tuple-element.37), channel_id=1, source_target_pairs={{0,2},{1,3},{2,0},{3,1},{4,6},{5,7},{6,4},{7,5},{8,10},{9,11},{10,... | collective-permute-start | bytes 147464 | tf_op jit(solution)/shard_map/ppermute | solution.py:27
  62.6 0.0 collective-permute-done.3.a3
  62.6 0.8 collective-permute-start.8
  63.4 0.0 collective-permute-done.4.a2
  63.4 0.0 collective-permute-done.5.a1
  63.4 0.0 copy-done.8
  63.4 0.0 copy-done.6
  63.5 1.3 %shard_map.127 = (bf16[32,1024]{1,0:T(8,128)(2,1)}, bf16[32,64,128]{2,1,0:T(8,128)(2,1)S(1)}) custom-call(bf16[32,128]{1,0:T(8,128)(2,1)S(1)} %collective-permute-done.3.a3, bf16[32,128]{1,0:T(8,128)(2,1)S(1)} %collective-permute-done.4.a2, bf16[32,128]{1,0:T(8,128)(2,1)S(1)} %collective-permute-done.5.a1, bf16[32,128]{1,0:T(8,128)(2,1)S(1)} %get-tuple-element.34.a0, ...), custom_call_target="tpu_custom_call" | custom-call | flops 1000000000 | bytes 3256320 | tf_op jit(solution)/shard_map/pallas_call | solution.py:291
  64.8 0.4 collective-permute-done.6.refs_0_
  65.2 0.0 collective-permute-done.7.refs_1_
  65.2 0.0 collective-permute-done.8.refs_0_
  65.2 16.5 %all_to_all.22.got_ref = bf16[32,64,128]{2,1,0:T(8,128)(2,1)S(1)} all-to-all(bf16[32,64,128]{2,1,0:T(8,128)(2,1)S(1)} %get-tuple-element.40), channel_id=1, replica_groups=mesh['ba'=8,'aa_0'=4,'aa_1'=4,'aa_2'=2] {'aa_0','aa_1','aa_2'}, dimensions={0} | all-to-all | bytes 1048576 | tf_op jit(solution)/shard_map/all_to_all | solution.py:312
  81.7 1.0 %shard_map.131 = (bf16[192,128]{1,0:T(8,128)(2,1)S(1)}, bf16[192,128]{1,0:T(8,128)(2,1)S(1)}) custom-call(bf16[32,64,128]{2,1,0:T(8,128)(2,1)S(1)} %all_to_all.22.got_ref, bf16[192,128]{1,0:T(8,128)(2,1)S(1)} %collective-permute-done.6.refs_0_, bf16[192,128]{1,0:T(8,128)(2,1)S(1)} %collective-permute-done.7.refs_1_), custom_call_target="tpu_custom_call" | custom-call | flops 1000000000 | bytes 622592 | tf_op jit(solution)/shard_map/pallas_call | solution.py:291
  82.7 0.2 collective-permute-start.10
  82.9 1.2 %collective-permute-start.11 = (bf16[192,128]{1,0:T(8,128)(2,1)S(1)}, bf16[192,128]{1,0:T(8,128)(2,1)S(1)}, u32[]{:S(2)}, u32[]{:S(2)}) collective-permute-start(bf16[192,128]{1,0:T(8,128)(2,1)S(1)} %get-tuple-element.46), channel_id=1, source_target_pairs={{0,3},{1,2},{2,1},{3,0},{4,7},{5,6},{6,5},{7,4},{8,11},{9,10},{10,... | collective-permute-start | bytes 147464 | tf_op jit(solution)/shard_map/ppermute | solution.py:27
  84.2 0.7 shard_map.130
  84.8 0.0 copy-start.9
  84.9 0.6 collective-permute-start.9
  85.4 0.7 shard_map.129.a0
  86.1 0.3 collective-permute-done.10.a2
  86.4 1.1 %collective-permute-done.11.a3 = bf16[192,128]{1,0:T(8,128)(2,1)S(1)} collective-permute-done((bf16[192,128]{1,0:T(8,128)(2,1)S(1)}, bf16[192,128]{1,0:T(8,128)(2,1)S(1)}, u32[]{:S(2)}, u32[]{:S(2)}) %collective-permute-start.11) | collective-permute-done | bytes 49184 | tf_op jit(solution)/shard_map/ppermute | solution.py:27
  87.4 0.0 collective-permute-done.9.a1
  87.4 0.0 copy-done.9
  87.4 1.1 %shard_map.132 = bf16[192,1024]{1,0:T(8,128)(2,1)} custom-call(bf16[192,128]{1,0:T(8,128)(2,1)S(1)} %shard_map.129.a0, bf16[192,128]{1,0:T(8,128)(2,1)S(1)} %collective-permute-done.9.a1, bf16[192,128]{1,0:T(8,128)(2,1)S(1)} %collective-permute-done.10.a2, bf16[192,128]{1,0:T(8,128)(2,1)S(1)} %collective-permute-done.11.a3, bf16[192,1024]{1,0:T(8,128)(2,1)S(1)} %copy-done.3, ...), custom_call_target="tpu_custom_call" | custom-call | flops 1000000000 | bytes 1638400 | tf_op jit(solution)/shard_map/pallas_call | solution.py:291
Async XLA Ops:
  3.6 33.7 %copy-start.1 = (bf16[512,1024]{1,0:T(8,128)(2,1)S(1)}, bf16[512,1024]{1,0:T(8,128)(2,1)}, u32[]{:S(2)}) copy-start(bf16[512,1024]{1,0:T(8,128)(2,1)} %wo_ref.3) | copy-start | bytes 3145732
  23.7 13.6 %copy-start = (bf16[1024,1536]{1,0:T(8,128)(2,1)S(1)}, bf16[1024,1536]{1,0:T(8,128)(2,1)}, u32[]{:S(2)}) copy-start(bf16[1024,1536]{1,0:T(8,128)(2,1)} %wqkv_ref.3) | copy-start | bytes 9437188
  23.7 13.6 %copy-start.4 = (bf16[32,1024]{1,0:T(8,128)(2,1)S(1)}, bf16[32,1024]{1,0:T(8,128)(2,1)}, u32[]{:S(2)}) copy-start(bf16[32,1024]{1,0:T(8,128)(2,1)} %latents_ref.1) | copy-start | bytes 196612
  23.7 13.6 %copy-start.5 = (f32[6,512]{1,0:T(8,128)S(1)}, f32[6,512]{1,0:T(8,128)}, u32[]{:S(2)}) copy-start(f32[6,512]{1,0:T(8,128)} %gain_ref.7) | copy-start | bytes 36868
  38.4 0.8 copy-start.2
  39.2 16.3 %all-to-all-start.2 = ((bf16[32,64,128]{2,1,0:T(8,128)(2,1)}), bf16[32,64,128]{2,1,0:T(8,128)(2,1)}, u32[]{:S(2)}, u32[]{:S(2)}) async-start(bf16[32,64,128]{2,1,0:T(8,128)(2,1)} %copy-done.2), calls=%async_computation.2 | async-start | bytes 1048576 | tf_op jit(solution)/shard_map/all_to_all | solution.py:312
  44.2 15.2 %copy-start.3 = (bf16[192,1024]{1,0:T(8,128)(2,1)S(1)}, bf16[192,1024]{1,0:T(8,128)(2,1)}, u32[]{:S(2)}) copy-start(bf16[192,1024]{1,0:T(8,128)(2,1)} %tokens_ref.3) | copy-start | bytes 1179652
  44.2 3.8 %collective-permute-start = (bf16[32,128]{1,0:T(8,128)(2,1)S(1)}, bf16[32,128]{1,0:T(8,128)(2,1)S(1)}, u32[]{:S(2)}, u32[]{:S(2)}) collective-permute-start(bf16[32,128]{1,0:T(8,128)(2,1)S(1)} %get-tuple-element.27), channel_id=1, source_target_pairs={{0,3},{1,2},{2,1},{3,0},{4,7},{5,6},{6,5},{7,4},{8,11},{9,10},{10,... | collective-permute-start | bytes 24584 | tf_op jit(solution)/shard_map/ppermute | solution.py:27
  45.9 3.2 %collective-permute-start.1 = (bf16[32,128]{1,0:T(8,128)(2,1)S(1)}, bf16[32,128]{1,0:T(8,128)(2,1)S(1)}, u32[]{:S(2)}, u32[]{:S(2)}) collective-permute-start(bf16[32,128]{1,0:T(8,128)(2,1)S(1)} %get-tuple-element.28), channel_id=1, source_target_pairs={{0,2},{1,3},{2,0},{3,1},{4,6},{5,7},{6,4},{7,5},{8,10},{9,11},{10,... | collective-permute-start | bytes 24584 | tf_op jit(solution)/shard_map/ppermute | solution.py:27
  46.0 3.1 %collective-permute-start.2 = (bf16[32,128]{1,0:T(8,128)(2,1)S(1)}, bf16[32,128]{1,0:T(8,128)(2,1)S(1)}, u32[]{:S(2)}, u32[]{:S(2)}) collective-permute-start(bf16[32,128]{1,0:T(8,128)(2,1)S(1)} %get-tuple-element.29), channel_id=1, source_target_pairs={{0,1},{1,0},{2,3},{3,2},{4,5},{5,4},{6,7},{7,6},{8,9},{9,8},{10,11... | collective-permute-start | bytes 24584 | tf_op jit(solution)/shard_map/ppermute | solution.py:27
  55.4 8.0 %copy-start.8 = (bf16[512,1024]{1,0:T(8,128)(2,1)S(1)}, bf16[512,1024]{1,0:T(8,128)(2,1)}, u32[]{:S(2)}) copy-start(bf16[512,1024]{1,0:T(8,128)(2,1)} %wo_ref.4) | copy-start | bytes 3145732
  57.1 6.4 %copy-start.6 = (bf16[1024,1024]{1,0:T(8,128)(2,1)S(1)}, bf16[1024,1024]{1,0:T(8,128)(2,1)}, u32[]{:S(2)}) copy-start(bf16[1024,1024]{1,0:T(8,128)(2,1)} %wkv_ref.1) | copy-start | bytes 6291460
  57.1 5.5 %collective-permute-start.3 = (bf16[32,128]{1,0:T(8,128)(2,1)S(1)}, bf16[32,128]{1,0:T(8,128)(2,1)S(1)}, u32[]{:S(2)}, u32[]{:S(2)}) collective-permute-start(bf16[32,128]{1,0:T(8,128)(2,1)S(1)} %get-tuple-element.31), channel_id=1, source_target_pairs={{0,3},{1,2},{2,1},{3,0},{4,7},{5,6},{6,5},{7,4},{8,11},{9,10},{10,... | collective-permute-start | bytes 24584 | tf_op jit(solution)/shard_map/ppermute | solution.py:27
  57.2 6.2 %collective-permute-start.4 = (bf16[32,128]{1,0:T(8,128)(2,1)S(1)}, bf16[32,128]{1,0:T(8,128)(2,1)S(1)}, u32[]{:S(2)}, u32[]{:S(2)}) collective-permute-start(bf16[32,128]{1,0:T(8,128)(2,1)S(1)} %get-tuple-element.32), channel_id=1, source_target_pairs={{0,2},{1,3},{2,0},{3,1},{4,6},{5,7},{6,4},{7,5},{8,10},{9,11},{10,... | collective-permute-start | bytes 24584 | tf_op jit(solution)/shard_map/ppermute | solution.py:27
  58.2 5.2 %collective-permute-start.5 = (bf16[32,128]{1,0:T(8,128)(2,1)S(1)}, bf16[32,128]{1,0:T(8,128)(2,1)S(1)}, u32[]{:S(2)}, u32[]{:S(2)}) collective-permute-start(bf16[32,128]{1,0:T(8,128)(2,1)S(1)} %get-tuple-element.33), channel_id=1, source_target_pairs={{0,1},{1,0},{2,3},{3,2},{4,5},{5,4},{6,7},{7,6},{8,9},{9,8},{10,11... | collective-permute-start | bytes 24584 | tf_op jit(solution)/shard_map/ppermute | solution.py:27
  59.3 1.2 %copy-start.7 = (bf16[1024,512]{1,0:T(8,128)(2,1)S(1)}, bf16[1024,512]{1,0:T(8,128)(2,1)}, u32[]{:S(2)}) copy-start(bf16[1024,512]{1,0:T(8,128)(2,1)} %wwq_ref.1) | copy-start | bytes 3145732
  61.2 4.0 %collective-permute-start.6 = (bf16[192,128]{1,0:T(8,128)(2,1)S(1)}, bf16[192,128]{1,0:T(8,128)(2,1)S(1)}, u32[]{:S(2)}, u32[]{:S(2)}) collective-permute-start(bf16[192,128]{1,0:T(8,128)(2,1)S(1)} %get-tuple-element.36), channel_id=1, source_target_pairs={{0,3},{1,2},{2,1},{3,0},{4,7},{5,6},{6,5},{7,4},{8,11},{9,10},{10,... | collective-permute-start | bytes 147464 | tf_op jit(solution)/shard_map/ppermute | solution.py:27
  61.3 3.9 %collective-permute-start.7 = (bf16[192,128]{1,0:T(8,128)(2,1)S(1)}, bf16[192,128]{1,0:T(8,128)(2,1)S(1)}, u32[]{:S(2)}, u32[]{:S(2)}) collective-permute-start(bf16[192,128]{1,0:T(8,128)(2,1)S(1)} %get-tuple-element.37), channel_id=1, source_target_pairs={{0,2},{1,3},{2,0},{3,1},{4,6},{5,7},{6,4},{7,5},{8,10},{9,11},{10,... | collective-permute-start | bytes 147464 | tf_op jit(solution)/shard_map/ppermute | solution.py:27
  62.6 2.5 %collective-permute-start.8 = (bf16[192,128]{1,0:T(8,128)(2,1)S(1)}, bf16[192,128]{1,0:T(8,128)(2,1)S(1)}, u32[]{:S(2)}, u32[]{:S(2)}) collective-permute-start(bf16[192,128]{1,0:T(8,128)(2,1)S(1)} %get-tuple-element.38), channel_id=1, source_target_pairs={{0,1},{1,0},{2,3},{3,2},{4,5},{5,4},{6,7},{7,6},{8,9},{9,8},{10,11... | collective-permute-start | bytes 147464 | tf_op jit(solution)/shard_map/ppermute | solution.py:27
  82.7 3.7 %collective-permute-start.10 = (bf16[192,128]{1,0:T(8,128)(2,1)S(1)}, bf16[192,128]{1,0:T(8,128)(2,1)S(1)}, u32[]{:S(2)}, u32[]{:S(2)}) collective-permute-start(bf16[192,128]{1,0:T(8,128)(2,1)S(1)} %get-tuple-element.45), channel_id=1, source_target_pairs={{0,2},{1,3},{2,0},{3,1},{4,6},{5,7},{6,4},{7,5},{8,10},{9,11},{10,... | collective-permute-start | bytes 147464 | tf_op jit(solution)/shard_map/ppermute | solution.py:27
  82.9 4.5 %collective-permute-start.11 = (bf16[192,128]{1,0:T(8,128)(2,1)S(1)}, bf16[192,128]{1,0:T(8,128)(2,1)S(1)}, u32[]{:S(2)}, u32[]{:S(2)}) collective-permute-start(bf16[192,128]{1,0:T(8,128)(2,1)S(1)} %get-tuple-element.46), channel_id=1, source_target_pairs={{0,3},{1,2},{2,1},{3,0},{4,7},{5,6},{6,5},{7,4},{8,11},{9,10},{10,... | collective-permute-start | bytes 147464 | tf_op jit(solution)/shard_map/ppermute | solution.py:27
  84.8 2.6 %copy-start.9 = (bf16[512,1024]{1,0:T(8,128)(2,1)S(1)}, bf16[512,1024]{1,0:T(8,128)(2,1)}, u32[]{:S(2)}) copy-start(bf16[512,1024]{1,0:T(8,128)(2,1)} %wo_ref.5) | copy-start | bytes 3145732
  84.9 2.6 %collective-permute-start.9 = (bf16[192,128]{1,0:T(8,128)(2,1)S(1)}, bf16[192,128]{1,0:T(8,128)(2,1)S(1)}, u32[]{:S(2)}, u32[]{:S(2)}) collective-permute-start(bf16[192,128]{1,0:T(8,128)(2,1)S(1)} %shard_map.130), channel_id=1, source_target_pairs={{0,1},{1,0},{2,3},{3,2},{4,5},{5,4},{6,7},{7,6},{8,9},{9,8},{10,11... | collective-permute-start | bytes 147464 | tf_op jit(solution)/shard_map/ppermute | solution.py:27

commit v2 on v1

--- a/solution.py
+++ b/solution.py
@@ -172,7 +172,7 @@
     count = rows - 16
     kv = got_ref[:, :count, :].reshape(devices * count, 128)
     kv1 = with_ones(kv, low_lanes(kv.shape))
-    step = 8
+    step = 16
     for at in range(0, devices, step):
         packed = got_ref[at : at + step, count:, :].reshape(step * 16, 128).astype(F32)
         low = low_lanes(packed.shape)
@@ -226,9 +226,14 @@
         send_ref[d, count:] = pair_of(values, d % PAIRS)
 
 
-def self_query_kernel(rows_ref, wqkv_ref, gain_ref, o0, o1, o2, o3, blocks_ref):
+def self_query_kernel(
+    rows_ref, wqkv_hbm, gain_ref, o0, o1, o2, o3, blocks_ref, wq_ref, sems
+):
+    copy = pltpu.make_async_copy(wqkv_hbm.at[:, :512], wq_ref, sems.at[0])
+    copy.start()
     normed = rms_rows(rows_ref[...].astype(F32))
-    queries = matmul(normed, wqkv_ref[:, :512])
+    copy.wait()
+    queries = matmul(normed, wq_ref[...])
     queries = head_norm(queries, gain_ref[2:3, :] * QUERY_SCALE).astype(BF16)
     for p in range(PAIRS):
         blocks_ref[p] = pair_of(queries, p)
@@ -281,17 +286,23 @@
     out_ref[...] = (tokens_ref[...].astype(F32) + update).astype(BF16)
 
 
-def call(body, outs, *args, scratch=(), fetch=None):
+def call(body, outs, *args, scratch=(), fetch=None, far=()):
     space = pltpu.HBM if fetch else pltpu.VMEM
     scratch = list(scratch)
     if fetch:
         scratch += [pltpu.VMEM(a.shape, a.dtype) for a in args]
         scratch.append(pltpu.SemaphoreType.DMA((len(args) + fetch,)))
         args = [pltpu.with_memory_space_constraint(a, space) for a in args]
+    args = [
+        pltpu.with_memory_space_constraint(a, pltpu.HBM) if i in far else a
+        for i, a in enumerate(args)
+    ]
     results = pl.pallas_call(
         body,
         out_shape=tuple(jax.ShapeDtypeStruct(s, BF16) for s in outs),
-        in_specs=[pl.BlockSpec(memory_space=space)] * len(args),
+        in_specs=[
+            pl.BlockSpec(memory_space=pltpu.HBM if i in far else space) for i in range(len(args))
+        ],
         out_specs=tuple(pl.BlockSpec(memory_space=pltpu.VMEM) for _ in outs),
         scratch_shapes=scratch,
         compiler_params=pltpu.CompilerParams(vmem_limit_bytes=48 * 1024 * 1024),
@@ -357,7 +368,9 @@
         own_rows,
         self_qkv,
         qk_gain,
-        scratch=blocks(rows),
+        scratch=blocks(rows)
+        + [pltpu.VMEM((1024, 512), BF16), pltpu.SemaphoreType.DMA((1,))],
+        far=(1,),
     )
     asked = call(
         write_query_kernel,

time: 89 us -> 86 us (0.966)
  local copies, waits for them, and re-layouts: 2.07 us -> 0.05 us
  waiting for transfers between devices: 10.7 us -> 9.49 us
  Pallas kernels: 13.5 us -> 14.4 us
    unnamed x20 -> x18, local copies, waits for them, and re-layouts: 2.07 us -> 0.05 us
    all_to_all x1, waiting for transfers between devices: 6.29 us -> 5.07 us  [all_to_all(): return lax.all_to_all(x, AA, split_axis=0, concat_axis=0, tiled=True)]
    pallas_call x11, Pallas kernels: 13.5 us -> 14.4 us  [call(): pl.pallas_call(body, out_shape=tuple((jax.ShapeDtypeStruct(s, BF16) for s...]
  transfers between devices with their start and end apart: 13 -> 13, of which waited for: 6 -> 6; matrix products, arithmetic and copies ran while one was open for 0% -> 0% of each run, Pallas kernels for 4% -> 6%
where the time goes in v2:
time: 86 us; the launch traced here: 85.6 us
  blocking collectives  48.3 us (56%)
  Pallas kernels  14.4 us (17%)
  starting transfers between devices  12.6 us (15%)
  waiting for transfers between devices  9.49 us (11%)
    all_to_all x3, blocking collectives, all_to_all(): return lax.all_to_all(x, AA, split_axis=0, concat_axis=0, tiled=True)  48.3 us
    pallas_call x11, Pallas kernels, call(): pl.pallas_call(body, out_shape=tuple((jax.ShapeDtypeStruct(s, BF16) for s...  14.4 us
    ppermute x12, starting transfers between devices, to_peer(): return lax.ppermute(x, ('aa_1', 'aa_2'), swaps)  8.72 us
    all_to_all x1, waiting for transfers between devices, all_to_all(): return lax.all_to_all(x, AA, split_axis=0, concat_axis=0, tiled=True)  5.07 us
    ppermute x12, waiting for transfers between devices, to_peer(): return lax.ppermute(x, ('aa_1', 'aa_2'), swaps)  4.42 us
    all_to_all x1, starting transfers between devices, all_to_all(): return lax.all_to_all(x, AA, split_axis=0, concat_axis=0, tiled=True)  3.84 us
  transfers between devices with their start and end apart: 13, of which 6 were waited for; matrix products, arithmetic and copies ran while one was open for 0% of the time, Pallas kernels for 6%

profile of v2, /device:TPU:1, one launch (start us, length us, event | category | flops | bytes accessed | tf_op | source)
XLA Modules:
  0.0 85.6 jit_solution(11860058514772373992)
XLA Ops:
  0.6 2.9 %shard_map.122 = bf16[32,64,128]{2,1,0:T(8,128)(2,1)S(1)} custom-call(bf16[192,1024]{1,0:T(8,128)(2,1)} %tokens_ref.3, bf16[32,1024]{1,0:T(8,128)(2,1)} %latents_ref.1, bf16[1024,512]{1,0:T(8,128)(2,1)} %wq_hbm.1, bf16[1024,1024]{1,0:T(8,128)(2,1)} %wkv_hbm.1, f32[6,512]{1,0:T(8,128)} %gain_ref.7), custom_call_target="tpu_custom_call" | custom-call | flops 1000000000 | bytes 3616768 | tf_op jit(solution)/shard_map/pallas_call | solution.py:300
  3.6 0.0 copy-start.1
  3.6 20.1 %all_to_all.20.got_ref = bf16[32,64,128]{2,1,0:T(8,128)(2,1)S(1)} all-to-all(bf16[32,64,128]{2,1,0:T(8,128)(2,1)S(1)} %shard_map.122), channel_id=1, replica_groups=mesh['ba'=8,'aa_0'=4,'aa_1'=4,'aa_2'=2] {'aa_0','aa_1','aa_2'}, dimensions={0} | all-to-all | bytes 1048576 | tf_op jit(solution)/shard_map/all_to_all | solution.py:323
  23.7 0.0 copy-start
  23.7 0.0 copy-start.3
  23.7 0.0 copy-start.4
  23.7 2.0 %shard_map.123 = bf16[32,24,128]{2,1,0:T(8,128)(2,1)S(1)} custom-call(bf16[32,64,128]{2,1,0:T(8,128)(2,1)S(1)} %all_to_all.20.got_ref), custom_call_target="tpu_custom_call" | custom-call | flops 1000000000 | bytes 524288 | tf_op jit(solution)/shard_map/pallas_call | solution.py:300
  25.7 11.7 %all_to_all.21.got_ref = bf16[32,24,128]{2,1,0:T(8,128)(2,1)S(1)} all-to-all(bf16[32,24,128]{2,1,0:T(8,128)(2,1)S(1)} %shard_map.123), channel_id=1, replica_groups=mesh['ba'=8,'aa_0'=4,'aa_1'=4,'aa_2'=2] {'aa_0','aa_1','aa_2'}, dimensions={0} | all-to-all | bytes 393216 | tf_op jit(solution)/shard_map/all_to_all | solution.py:323
  37.4 0.0 copy-done.1
  37.4 0.0 copy-done
  37.4 0.0 copy-done.3
  37.4 0.0 copy-done.4
  37.4 1.8 %shard_map.124 = (bf16[32,1024]{1,0:T(8,128)(2,1)S(1)}, bf16[32,64,128]{2,1,0:T(8,128)(2,1)}) custom-call(bf16[32,24,128]{2,1,0:T(8,128)(2,1)S(1)} %all_to_all.21.got_ref, bf16[32,1024]{1,0:T(8,128)(2,1)S(1)} %copy-done.3, bf16[512,1024]{1,0:T(8,128)(2,1)S(1)} %copy-done.1, bf16[1024,1536]{1,0:T(8,128)(2,1)S(1)} %copy-done, f32[6,512]{1,0:T(8,128)S(1)} %copy-done.4), custom_call_target="tpu_custom_call" | custom-call | flops 1000000000 | bytes 4468736 | tf_op jit(solution)/shard_map/pallas_call | solution.py:300
  39.3 3.8 %all-to-all-start.2 = ((bf16[32,64,128]{2,1,0:T(8,128)(2,1)}), bf16[32,64,128]{2,1,0:T(8,128)(2,1)S(1)}, u32[]{:S(2)}, u32[]{:S(2)}) async-start(bf16[32,64,128]{2,1,0:T(8,128)(2,1)} %get-tuple-element.25), calls=%async_computation.2 | async-start | bytes 1048576 | tf_op jit(solution)/shard_map/all_to_all | solution.py:323
  43.1 1.7 %shard_map.125 = (bf16[32,128]{1,0:T(8,128)(2,1)S(1)}, bf16[32,128]{1,0:T(8,128)(2,1)S(1)}, bf16[32,128]{1,0:T(8,128)(2,1)S(1)}, bf16[32,128]{1,0:T(8,128)(2,1)S(1)}) custom-call(bf16[32,1024]{1,0:T(8,128)(2,1)S(1)} %get-tuple-element.26.rows_ref, bf16[1024,1536]{1,0:T(8,128)(2,1)} %wqkv_hbm.1, f32[6,512]{1,0:T(8,128)S(1)} %copy-done.4), custom_call_target="tpu_custom_call" | custom-call | flops 1000000000 | bytes 3223552 | tf_op jit(solution)/shard_map/pallas_call | solution.py:300
  44.8 0.0 copy-start.2
  44.8 0.0 copy-start.6
  44.8 1.7 %collective-permute-start = (bf16[32,128]{1,0:T(8,128)(2,1)S(1)}, bf16[32,128]{1,0:T(8,128)(2,1)S(1)}, u32[]{:S(2)}, u32[]{:S(2)}) collective-permute-start(bf16[32,128]{1,0:T(8,128)(2,1)S(1)} %get-tuple-element.27), channel_id=1, source_target_pairs={{0,3},{1,2},{2,1},{3,0},{4,7},{5,6},{6,5},{7,4},{8,11},{9,10},{10,... | collective-permute-start | bytes 24584 | tf_op jit(solution)/shard_map/ppermute | solution.py:27
  46.5 0.1 collective-permute-start.1
  46.6 0.4 collective-permute-start.2
  47.0 1.5 %collective-permute-done.refs_0_ = bf16[32,128]{1,0:T(8,128)(2,1)S(1)} collective-permute-done((bf16[32,128]{1,0:T(8,128)(2,1)S(1)}, bf16[32,128]{1,0:T(8,128)(2,1)S(1)}, u32[]{:S(2)}, u32[]{:S(2)}) %collective-permute-start) | collective-permute-done | bytes 8224 | tf_op jit(solution)/shard_map/ppermute | solution.py:27
  48.5 1.2 %collective-permute-done.1.refs_1_ = bf16[32,128]{1,0:T(8,128)(2,1)S(1)} collective-permute-done((bf16[32,128]{1,0:T(8,128)(2,1)S(1)}, bf16[32,128]{1,0:T(8,128)(2,1)S(1)}, u32[]{:S(2)}, u32[]{:S(2)}) %collective-permute-start.1) | collective-permute-done | bytes 8224 | tf_op jit(solution)/shard_map/ppermute | solution.py:27
  49.7 0.0 collective-permute-done.2.refs_2_
  49.7 5.1 %all-to-all-done.2.got_ref = bf16[32,64,128]{2,1,0:T(8,128)(2,1)S(1)} async-done(((bf16[32,64,128]{2,1,0:T(8,128)(2,1)}), bf16[32,64,128]{2,1,0:T(8,128)(2,1)S(1)}, u32[]{:S(2)}, u32[]{:S(2)}) %all-to-all-start.2) | async-done | bytes 524320 | tf_op jit(solution)/shard_map/all_to_all | solution.py:323
  54.8 0.5 shard_map.126
  55.3 0.0 copy-start.5
  55.3 0.0 copy-start.7
  55.4 0.2 collective-permute-start.3
  55.5 1.0 %collective-permute-start.4 = (bf16[32,128]{1,0:T(8,128)(2,1)S(1)}, bf16[32,128]{1,0:T(8,128)(2,1)S(1)}, u32[]{:S(2)}, u32[]{:S(2)}) collective-permute-start(bf16[32,128]{1,0:T(8,128)(2,1)S(1)} %get-tuple-element.32), channel_id=1, source_target_pairs={{0,2},{1,3},{2,0},{3,1},{4,6},{5,7},{6,4},{7,5},{8,10},{9,11},{10,... | collective-permute-start | bytes 24584 | tf_op jit(solution)/shard_map/ppermute | solution.py:27
  56.5 1.1 %collective-permute-start.5 = (bf16[32,128]{1,0:T(8,128)(2,1)S(1)}, bf16[32,128]{1,0:T(8,128)(2,1)S(1)}, u32[]{:S(2)}, u32[]{:S(2)}) collective-permute-start(bf16[32,128]{1,0:T(8,128)(2,1)S(1)} %get-tuple-element.33), channel_id=1, source_target_pairs={{0,1},{1,0},{2,3},{3,2},{4,5},{5,4},{6,7},{7,6},{8,9},{9,8},{10,11... | collective-permute-start | bytes 24584 | tf_op jit(solution)/shard_map/ppermute | solution.py:27
  57.6 0.0 copy-done.2
  57.6 0.0 copy-done.6
  57.6 0.6 shard_map.128
  58.3 0.1 collective-permute-start.6
  58.4 1.3 %collective-permute-start.7 = (bf16[192,128]{1,0:T(8,128)(2,1)S(1)}, bf16[192,128]{1,0:T(8,128)(2,1)S(1)}, u32[]{:S(2)}, u32[]{:S(2)}) collective-permute-start(bf16[192,128]{1,0:T(8,128)(2,1)S(1)} %get-tuple-element.37), channel_id=1, source_target_pairs={{0,2},{1,3},{2,0},{3,1},{4,6},{5,7},{6,4},{7,5},{8,10},{9,11},{10,... | collective-permute-start | bytes 147464 | tf_op jit(solution)/shard_map/ppermute | solution.py:27
  59.7 0.0 collective-permute-done.3.a3
  59.7 0.8 collective-permute-start.8
  60.5 0.0 collective-permute-done.4.a2
  60.5 0.0 collective-permute-done.5.a1
  60.5 0.0 copy-done.5
  60.5 0.0 copy-done.7
  60.5 1.3 %shard_map.127 = (bf16[32,1024]{1,0:T(8,128)(2,1)}, bf16[32,64,128]{2,1,0:T(8,128)(2,1)S(1)}) custom-call(bf16[32,128]{1,0:T(8,128)(2,1)S(1)} %collective-permute-done.3.a3, bf16[32,128]{1,0:T(8,128)(2,1)S(1)} %collective-permute-done.4.a2, bf16[32,128]{1,0:T(8,128)(2,1)S(1)} %collective-permute-done.5.a1, bf16[32,128]{1,0:T(8,128)(2,1)S(1)} %get-tuple-element.34.a0, ...), custom_call_target="tpu_custom_call" | custom-call | flops 1000000000 | bytes 3256320 | tf_op jit(solution)/shard_map/pallas_call | solution.py:300
  61.8 0.4 collective-permute-done.6.refs_0_
  62.2 0.0 collective-permute-done.7.refs_1_
  62.2 0.0 collective-permute-done.8.refs_0_
  62.2 16.5 %all_to_all.22.got_ref = bf16[32,64,128]{2,1,0:T(8,128)(2,1)S(1)} all-to-all(bf16[32,64,128]{2,1,0:T(8,128)(2,1)S(1)} %get-tuple-element.40), channel_id=1, replica_groups=mesh['ba'=8,'aa_0'=4,'aa_1'=4,'aa_2'=2] {'aa_0','aa_1','aa_2'}, dimensions={0} | all-to-all | bytes 1048576 | tf_op jit(solution)/shard_map/all_to_all | solution.py:323
  78.7 1.0 %shard_map.131 = (bf16[192,128]{1,0:T(8,128)(2,1)S(1)}, bf16[192,128]{1,0:T(8,128)(2,1)S(1)}) custom-call(bf16[32,64,128]{2,1,0:T(8,128)(2,1)S(1)} %all_to_all.22.got_ref, bf16[192,128]{1,0:T(8,128)(2,1)S(1)} %collective-permute-done.6.refs_0_, bf16[192,128]{1,0:T(8,128)(2,1)S(1)} %collective-permute-done.7.refs_1_), custom_call_target="tpu_custom_call" | custom-call | flops 1000000000 | bytes 622592 | tf_op jit(solution)/shard_map/pallas_call | solution.py:300
  79.8 0.2 collective-permute-start.10
  80.0 1.2 %collective-permute-start.11 = (bf16[192,128]{1,0:T(8,128)(2,1)S(1)}, bf16[192,128]{1,0:T(8,128)(2,1)S(1)}, u32[]{:S(2)}, u32[]{:S(2)}) collective-permute-start(bf16[192,128]{1,0:T(8,128)(2,1)S(1)} %get-tuple-element.46), channel_id=1, source_target_pairs={{0,3},{1,2},{2,1},{3,0},{4,7},{5,6},{6,5},{7,4},{8,11},{9,10},{10,... | collective-permute-start | bytes 147464 | tf_op jit(solution)/shard_map/ppermute | solution.py:27
  81.2 0.7 shard_map.130
  81.9 0.0 copy-start.8
  81.9 0.6 collective-permute-start.9
  82.5 0.7 shard_map.129.a0
  83.2 0.3 collective-permute-done.10.a2
  83.4 1.1 %collective-permute-done.11.a3 = bf16[192,128]{1,0:T(8,128)(2,1)S(1)} collective-permute-done((bf16[192,128]{1,0:T(8,128)(2,1)S(1)}, bf16[192,128]{1,0:T(8,128)(2,1)S(1)}, u32[]{:S(2)}, u32[]{:S(2)}) %collective-permute-start.11) | collective-permute-done | bytes 49184 | tf_op jit(solution)/shard_map/ppermute | solution.py:27
  84.5 0.0 collective-permute-done.9.a1
  84.5 0.0 copy-done.8
  84.5 1.1 %shard_map.132 = bf16[192,1024]{1,0:T(8,128)(2,1)} custom-call(bf16[192,128]{1,0:T(8,128)(2,1)S(1)} %shard_map.129.a0, bf16[192,128]{1,0:T(8,128)(2,1)S(1)} %collective-permute-done.9.a1, bf16[192,128]{1,0:T(8,128)(2,1)S(1)} %collective-permute-done.10.a2, bf16[192,128]{1,0:T(8,128)(2,1)S(1)} %collective-permute-done.11.a3, bf16[192,1024]{1,0:T(8,128)(2,1)S(1)} %copy-done.2, ...), custom_call_target="tpu_custom_call" | custom-call | flops 1000000000 | bytes 1638400 | tf_op jit(solution)/shard_map/pallas_call | solution.py:300
Async XLA Ops:
  3.6 33.8 %copy-start.1 = (bf16[512,1024]{1,0:T(8,128)(2,1)S(1)}, bf16[512,1024]{1,0:T(8,128)(2,1)}, u32[]{:S(2)}) copy-start(bf16[512,1024]{1,0:T(8,128)(2,1)} %wo_ref.3) | copy-start | bytes 3145732
  23.7 13.7 %copy-start = (bf16[1024,1536]{1,0:T(8,128)(2,1)S(1)}, bf16[1024,1536]{1,0:T(8,128)(2,1)}, u32[]{:S(2)}) copy-start(bf16[1024,1536]{1,0:T(8,128)(2,1)} %wqkv_hbm.1) | copy-start | bytes 9437188
  23.7 13.7 %copy-start.3 = (bf16[32,1024]{1,0:T(8,128)(2,1)S(1)}, bf16[32,1024]{1,0:T(8,128)(2,1)}, u32[]{:S(2)}) copy-start(bf16[32,1024]{1,0:T(8,128)(2,1)} %latents_ref.1) | copy-start | bytes 196612
  23.7 13.7 %copy-start.4 = (f32[6,512]{1,0:T(8,128)S(1)}, f32[6,512]{1,0:T(8,128)}, u32[]{:S(2)}) copy-start(f32[6,512]{1,0:T(8,128)} %gain_ref.7) | copy-start | bytes 36868
  39.3 15.6 %all-to-all-start.2 = ((bf16[32,64,128]{2,1,0:T(8,128)(2,1)}), bf16[32,64,128]{2,1,0:T(8,128)(2,1)S(1)}, u32[]{:S(2)}, u32[]{:S(2)}) async-start(bf16[32,64,128]{2,1,0:T(8,128)(2,1)} %get-tuple-element.25), calls=%async_computation.2 | async-start | bytes 1048576 | tf_op jit(solution)/shard_map/all_to_all | solution.py:323
  44.8 12.8 %copy-start.2 = (bf16[192,1024]{1,0:T(8,128)(2,1)S(1)}, bf16[192,1024]{1,0:T(8,128)(2,1)}, u32[]{:S(2)}) copy-start(bf16[192,1024]{1,0:T(8,128)(2,1)} %tokens_ref.3) | copy-start | bytes 1179652
  44.8 12.8 %copy-start.6 = (bf16[1024,512]{1,0:T(8,128)(2,1)S(1)}, bf16[1024,512]{1,0:T(8,128)(2,1)}, u32[]{:S(2)}) copy-start(bf16[1024,512]{1,0:T(8,128)(2,1)} %wwq_ref.1) | copy-start | bytes 3145732
  44.8 3.7 %collective-permute-start = (bf16[32,128]{1,0:T(8,128)(2,1)S(1)}, bf16[32,128]{1,0:T(8,128)(2,1)S(1)}, u32[]{:S(2)}, u32[]{:S(2)}) collective-permute-start(bf16[32,128]{1,0:T(8,128)(2,1)S(1)} %get-tuple-element.27), channel_id=1, source_target_pairs={{0,3},{1,2},{2,1},{3,0},{4,7},{5,6},{6,5},{7,4},{8,11},{9,10},{10,... | collective-permute-start | bytes 24584 | tf_op jit(solution)/shard_map/ppermute | solution.py:27
  46.5 3.2 %collective-permute-start.1 = (bf16[32,128]{1,0:T(8,128)(2,1)S(1)}, bf16[32,128]{1,0:T(8,128)(2,1)S(1)}, u32[]{:S(2)}, u32[]{:S(2)}) collective-permute-start(bf16[32,128]{1,0:T(8,128)(2,1)S(1)} %get-tuple-element.28), channel_id=1, source_target_pairs={{0,2},{1,3},{2,0},{3,1},{4,6},{5,7},{6,4},{7,5},{8,10},{9,11},{10,... | collective-permute-start | bytes 24584 | tf_op jit(solution)/shard_map/ppermute | solution.py:27
  46.6 3.1 %collective-permute-start.2 = (bf16[32,128]{1,0:T(8,128)(2,1)S(1)}, bf16[32,128]{1,0:T(8,128)(2,1)S(1)}, u32[]{:S(2)}, u32[]{:S(2)}) collective-permute-start(bf16[32,128]{1,0:T(8,128)(2,1)S(1)} %get-tuple-element.29), channel_id=1, source_target_pairs={{0,1},{1,0},{2,3},{3,2},{4,5},{5,4},{6,7},{7,6},{8,9},{9,8},{10,11... | collective-permute-start | bytes 24584 | tf_op jit(solution)/shard_map/ppermute | solution.py:27
  55.3 5.2 %copy-start.5 = (bf16[1024,1024]{1,0:T(8,128)(2,1)S(1)}, bf16[1024,1024]{1,0:T(8,128)(2,1)}, u32[]{:S(2)}) copy-start(bf16[1024,1024]{1,0:T(8,128)(2,1)} %wkv_ref.1) | copy-start | bytes 6291460
  55.3 5.1 %copy-start.7 = (bf16[512,1024]{1,0:T(8,128)(2,1)S(1)}, bf16[512,1024]{1,0:T(8,128)(2,1)}, u32[]{:S(2)}) copy-start(bf16[512,1024]{1,0:T(8,128)(2,1)} %wo_ref.4) | copy-start | bytes 3145732
  55.4 4.3 %collective-permute-start.3 = (bf16[32,128]{1,0:T(8,128)(2,1)S(1)}, bf16[32,128]{1,0:T(8,128)(2,1)S(1)}, u32[]{:S(2)}, u32[]{:S(2)}) collective-permute-start(bf16[32,128]{1,0:T(8,128)(2,1)S(1)} %get-tuple-element.31), channel_id=1, source_target_pairs={{0,3},{1,2},{2,1},{3,0},{4,7},{5,6},{6,5},{7,4},{8,11},{9,10},{10,... | collective-permute-start | bytes 24584 | tf_op jit(solution)/shard_map/ppermute | solution.py:27
  55.5 5.0 %collective-permute-start.4 = (bf16[32,128]{1,0:T(8,128)(2,1)S(1)}, bf16[32,128]{1,0:T(8,128)(2,1)S(1)}, u32[]{:S(2)}, u32[]{:S(2)}) collective-permute-start(bf16[32,128]{1,0:T(8,128)(2,1)S(1)} %get-tuple-element.32), channel_id=1, source_target_pairs={{0,2},{1,3},{2,0},{3,1},{4,6},{5,7},{6,4},{7,5},{8,10},{9,11},{10,... | collective-permute-start | bytes 24584 | tf_op jit(solution)/shard_map/ppermute | solution.py:27
  56.5 4.0 %collective-permute-start.5 = (bf16[32,128]{1,0:T(8,128)(2,1)S(1)}, bf16[32,128]{1,0:T(8,128)(2,1)S(1)}, u32[]{:S(2)}, u32[]{:S(2)}) collective-permute-start(bf16[32,128]{1,0:T(8,128)(2,1)S(1)} %get-tuple-element.33), channel_id=1, source_target_pairs={{0,1},{1,0},{2,3},{3,2},{4,5},{5,4},{6,7},{7,6},{8,9},{9,8},{10,11... | collective-permute-start | bytes 24584 | tf_op jit(solution)/shard_map/ppermute | solution.py:27
  58.3 4.0 %collective-permute-start.6 = (bf16[192,128]{1,0:T(8,128)(2,1)S(1)}, bf16[192,128]{1,0:T(8,128)(2,1)S(1)}, u32[]{:S(2)}, u32[]{:S(2)}) collective-permute-start(bf16[192,128]{1,0:T(8,128)(2,1)S(1)} %get-tuple-element.36), channel_id=1, source_target_pairs={{0,3},{1,2},{2,1},{3,0},{4,7},{5,6},{6,5},{7,4},{8,11},{9,10},{10,... | collective-permute-start | bytes 147464 | tf_op jit(solution)/shard_map/ppermute | solution.py:27
  58.4 3.9 %collective-permute-start.7 = (bf16[192,128]{1,0:T(8,128)(2,1)S(1)}, bf16[192,128]{1,0:T(8,128)(2,1)S(1)}, u32[]{:S(2)}, u32[]{:S(2)}) collective-permute-start(bf16[192,128]{1,0:T(8,128)(2,1)S(1)} %get-tuple-element.37), channel_id=1, source_target_pairs={{0,2},{1,3},{2,0},{3,1},{4,6},{5,7},{6,4},{7,5},{8,10},{9,11},{10,... | collective-permute-start | bytes 147464 | tf_op jit(solution)/shard_map/ppermute | solution.py:27
  59.7 2.5 %collective-permute-start.8 = (bf16[192,128]{1,0:T(8,128)(2,1)S(1)}, bf16[192,128]{1,0:T(8,128)(2,1)S(1)}, u32[]{:S(2)}, u32[]{:S(2)}) collective-permute-start(bf16[192,128]{1,0:T(8,128)(2,1)S(1)} %get-tuple-element.38), channel_id=1, source_target_pairs={{0,1},{1,0},{2,3},{3,2},{4,5},{5,4},{6,7},{7,6},{8,9},{9,8},{10,11... | collective-permute-start | bytes 147464 | tf_op jit(solution)/shard_map/ppermute | solution.py:27
  79.8 3.7 %collective-permute-start.10 = (bf16[192,128]{1,0:T(8,128)(2,1)S(1)}, bf16[192,128]{1,0:T(8,128)(2,1)S(1)}, u32[]{:S(2)}, u32[]{:S(2)}) collective-permute-start(bf16[192,128]{1,0:T(8,128)(2,1)S(1)} %get-tuple-element.45), channel_id=1, source_target_pairs={{0,2},{1,3},{2,0},{3,1},{4,6},{5,7},{6,4},{7,5},{8,10},{9,11},{10,... | collective-permute-start | bytes 147464 | tf_op jit(solution)/shard_map/ppermute | solution.py:27
  80.0 4.5 %collective-permute-start.11 = (bf16[192,128]{1,0:T(8,128)(2,1)S(1)}, bf16[192,128]{1,0:T(8,128)(2,1)S(1)}, u32[]{:S(2)}, u32[]{:S(2)}) collective-permute-start(bf16[192,128]{1,0:T(8,128)(2,1)S(1)} %get-tuple-element.46), channel_id=1, source_target_pairs={{0,3},{1,2},{2,1},{3,0},{4,7},{5,6},{6,5},{7,4},{8,11},{9,10},{10,... | collective-permute-start | bytes 147464 | tf_op jit(solution)/shard_map/ppermute | solution.py:27
  81.9 2.6 %copy-start.8 = (bf16[512,1024]{1,0:T(8,128)(2,1)S(1)}, bf16[512,1024]{1,0:T(8,128)(2,1)}, u32[]{:S(2)}) copy-start(bf16[512,1024]{1,0:T(8,128)(2,1)} %wo_ref.5) | copy-start | bytes 3145732
  81.9 2.6 %collective-permute-start.9 = (bf16[192,128]{1,0:T(8,128)(2,1)S(1)}, bf16[192,128]{1,0:T(8,128)(2,1)S(1)}, u32[]{:S(2)}, u32[]{:S(2)}) collective-permute-start(bf16[192,128]{1,0:T(8,128)(2,1)S(1)} %shard_map.130), channel_id=1, source_target_pairs={{0,1},{1,0},{2,3},{3,2},{4,5},{5,4},{6,7},{7,6},{8,9},{9,8},{10,11... | collective-permute-start | bytes 147464 | tf_op jit(solution)/shard_map/ppermute | solution.py:27
